TPU v7x, 32 devices: a whole 2x2x4 slice. The times are simulated.
32 devices in a mesh: chip: 8 (over y, x, core), line: 4 (over z).
Axes of the slice: x: 2, y: 2, z: 4, core: 2. Of those that a mesh axis runs over, the one named last changes fastest.
Arguments:
- echoes: bfloat16 [8, 2, 4096, 4096], P('chip', None, 'line'), may hold values from -6 to 6
- range_filter: float32 [2, 4096], replicated, may hold values from -6 to 6
- rcmc_weights: float32 [8, 4096], replicated, may hold values from -3 to 3
- fm_rate: float32 [8, 384], P('chip', 'line'), may hold values from 256 to 2048
- rcmc_shift: int32 [8, 384], P('chip', 'line'), may hold values from 0 to 12, as said below
- seam_width: int32 [8], P('chip'), may hold values from 64 to 128, as said below
- seam_link: int32 [8], P('chip'), may hold values from 0 to 1
Outputs:
- image: bfloat16 [8, 2, 384, 4096], P('chip', None, 'line')
Inputs may be any that keep to these rules, and one draw needn't show every extreme that they name: `rcmc_shift`: every draw has some entry equal to 12. `seam_width`: every draw has some chip with the width 128.
All inputs are finite; a program needn't handle non-finite values.
Results may differ from a plain program's by a relative error of at most 0.0011.
Values sent between devices are 32-bit elements; how exact they have to be, the bound alone decides.
No kernel may reach another device: no remote copies, remote signals or barrier semaphores. Data moves between devices by JAX's collectives and lax.ppermute only.
A program may use at most 192 MiB of HBM per device.

v0:
```python
import math

import jax
import jax.numpy as jnp
from jax import lax
from jax.sharding import PartitionSpec as P

RKEEP = 384
TAPS = 8
MAXSHIFT = 12
OVL = 128


def shifted(value, axis, steps):
    count = lax.axis_size(axis)
    initial, last = (max(0, -steps), min(count, count - steps))
    return lax.ppermute(value, axis, [(source, source + steps) for source in range(initial, last)])


def twiddle_table(length, rows, columns, sign):
    product = (
        lax.broadcasted_iota(jnp.int32, (rows, columns), 0)
        * lax.broadcasted_iota(jnp.int32, (rows, columns), 1)
        % length
    )
    angle = sign * 2.0 * math.pi / length * product.astype(jnp.float32)
    return (jnp.cos(angle), jnp.sin(angle))


def stacked_table(table):
    table_real, table_imag = table
    return jnp.stack([jnp.stack([table_real, table_imag]), jnp.stack([-table_imag, table_real])])


def complex_einsum(form, pair, table):
    return jnp.einsum(
        form,
        pair,
        stacked_table(table),
        precision=lax.Precision.HIGHEST,
        preferred_element_type=jnp.float32,
    )


def complex_scale(pair, factor):
    factor_real, factor_imag = factor
    return jnp.stack(
        [
            pair[0] * factor_real - pair[1] * factor_imag,
            pair[0] * factor_imag + pair[1] * factor_real,
        ]
    )


def split_length(length):
    inner = min(128, length)
    return (length // inner, inner)


def forward_transform(pair):
    length = pair.shape[-1]
    outer, inner = split_length(length)
    pair = pair.reshape(pair.shape[:-1] + (outer, inner))
    pair = complex_einsum("c...pq,cdpk->d...kq", pair, twiddle_table(outer, outer, outer, -1))
    pair = complex_scale(pair, twiddle_table(length, outer, inner, -1))
    return complex_einsum("c...kq,cdqm->d...km", pair, twiddle_table(inner, inner, inner, -1))


def inverse_transform(pair, keep, form):
    outer, inner = (pair.shape[-2], pair.shape[-1])
    length = outer * inner
    pair = complex_einsum("c...kq,cdqn->d...kn", pair, twiddle_table(inner, inner, inner, 1))
    pair = complex_scale(pair, twiddle_table(length, outer, inner, 1))
    table_real, table_imag = twiddle_table(outer, outer, keep // inner, 1)
    return complex_einsum(form, pair, (table_real / length, table_imag / length))


def local(echoes, range_filter, rcmc_weights, fm_rate, rcmc_shift, seam_width, seam_link):
    lines = echoes.shape[2]
    samples = echoes.shape[3]
    margin = MAXSHIFT + TAPS - 1
    raw = echoes[0].astype(jnp.float32)
    spectrum = forward_transform(raw)
    outer, inner = split_length(samples)
    filter_pair = (range_filter[0].reshape(inner, outer).T, range_filter[1].reshape(inner, outer).T)
    spectrum = complex_scale(spectrum, filter_pair)
    compressed = inverse_transform(spectrum, RKEEP, "clkn,cdkm->dmnl")
    gain = 1.0 + 2.0 * lax.broadcasted_iota(jnp.float32, (RKEEP, 1), 0) / RKEEP
    compressed = compressed.reshape(2, RKEEP, lines) * gain
    turned = lax.all_to_all(compressed, "line", split_axis=1, concat_axis=2, tiled=True)
    doppler = forward_transform(turned)
    below = shifted(doppler[:, :margin], "line", -1)
    extended = jnp.concatenate([doppler, below], axis=1)
    rows = extended.shape[1] - margin
    outer_az, inner_az = (extended.shape[2], extended.shape[3])
    length_az = outer_az * inner_az
    weights = rcmc_weights.reshape(TAPS, inner_az, outer_az).transpose(0, 2, 1)
    positions = lax.broadcasted_iota(jnp.int32, (rows,), 0) + rcmc_shift[0]
    migrated = jnp.zeros((2, rows, outer_az, inner_az), jnp.float32)
    for offset in range(TAPS):
        picked = jnp.take(extended, positions + offset, axis=1)
        migrated = migrated + weights[offset] * picked
    index = lax.broadcasted_iota(
        jnp.int32, (outer_az, inner_az), 0
    ) + outer_az * lax.broadcasted_iota(jnp.int32, (outer_az, inner_az), 1)
    frequency = ((index + length_az // 2) % length_az - length_az // 2).astype(
        jnp.float32
    ) / length_az
    phase = math.pi * (fm_rate[0][:, None, None] * (frequency * frequency)[None])
    focus = complex_scale(migrated, (jnp.cos(phase), -jnp.sin(phase)))
    image = inverse_transform(focus, length_az, "c...kn,cdkm->d...mn").reshape(2, rows, length_az)
    tail = image[:, :, length_az - OVL :]
    earlier = shifted(tail, "chip", 1)
    width = seam_width[0]
    linked = seam_link[0]
    offsets = lax.broadcasted_iota(jnp.int32, (OVL,), 0)
    columns = jnp.clip(OVL - width + offsets, 0, OVL - 1)
    previous = jnp.take(earlier, columns, axis=2)
    ramp = (offsets.astype(jnp.float32) + 0.5) / width.astype(jnp.float32)
    inside = (offsets < width) & (linked == 1)
    head = image[:, :, :OVL]
    mixed = jnp.where(inside, (1.0 - ramp) * previous + ramp * head, head)
    blended = jnp.concatenate([mixed, image[:, :, OVL:]], axis=2)
    energy = lax.psum(jnp.sum(blended * blended), "line")
    scale = lax.rsqrt(energy / (RKEEP * length_az) + 1e-06)
    return (blended * scale).astype(jnp.bfloat16)[None]


def solution(mesh):
    in_specs = (
        P("chip", None, "line", None),
        P(),
        P(),
        P("chip", "line"),
        P("chip", "line"),
        P("chip"),
        P("chip"),
    )
    out_specs = P("chip", None, "line", None)
    return jax.shard_map(local, mesh=mesh, in_specs=in_specs, out_specs=out_specs, check_vma=False)
```

profile of v0, /device:TPU:12, one launch (start us, length us, event | category | flops | bytes accessed | tf_op | source)
XLA Modules:
  0.0 522.4 jit_solution(14466123838629571544)
XLA Ops:
  3.3 15.1 %copy.148 = bf16[256,8,32,128]{3,2,1,0:T(8,128)(2,1)} copy(bf16[256,8,32,128]{3,1,2,0:T(8,128)(2,1)} %bitcast.264) | data formatting | bytes 33554432
  18.9 22.6 %convolution_bitcast_fusion = f32[2,1024,32,128]{3,2,1,0:T(8,128)} fusion(f32[1,2,32,32]{2,3,0,1:T(8,128)S(1)} %get-tuple-element.53, f32[1,2,32,32]{2,3,0,1:T(8,128)S(1)} %get-tuple-element.52, bf16[2,1024,32,128]{3,2,1,0:T(8,128)(2,1)} %bitcast.263), kind=kOutput, calls=%fused_computation.19 | convolution fusion | flops 6442455040 | bytes 50348032 | tf_op jit(solution)/shard_map/c...pq,cdpk->d...kq/dot_general | solution.py:36
  41.5 18.0 %multiply_subtract_fusion.2 = (f32[1,1024,32,128]{3,2,1,0:T(8,128)S(1)}, f32[1,1024,32,128]{3,2,1,0:T(8,128)}) fusion(f32[2,1024,32,128]{3,2,1,0:T(8,128)} %convolution_bitcast_fusion, f32[32,128]{1,0:T(8,128)S(1)} %get-tuple-element.72, f32[32,128]{1,0:T(8,128)S(1)} %get-tuple-element.73), kind=kLoop, calls=%fused_computation.29 | loop fusion | flops 25165824 | bytes 67141632 | tf_op jit(solution)/shard_map/sub | solution.py:49
  59.5 18.7 %pad_maximum_fusion = f32[2,1024,32,128]{3,2,1,0:T(8,128)} fusion(f32[1,1024,32,128]{3,2,1,0:T(8,128)} %get-tuple-element.27, f32[1,1024,32,128]{3,2,1,0:T(8,128)S(1)} %get-tuple-element.26), kind=kLoop, calls=%fused_computation.9 | loop fusion | flops 8388608 | bytes 67108864 | tf_op jit(solution)/shard_map/stack | solution.py:47
  78.9 67.2 %fusion.7 = f32[2,1024,32,128]{1,3,2,0:T(8,128)} fusion(f32[2,1024,32,128]{3,2,1,0:T(8,128)} %pad_maximum_fusion, f32[1,2,128,128]{2,3,0,1:T(8,128)S(1)} %get-tuple-element.49, f32[1,2,128,128]{2,3,0,1:T(8,128)S(1)} %get-tuple-element.48), kind=kOutput, calls=%fused_computation.20 | convolution fusion | flops 25769869312 | bytes 67371008 | tf_op jit(solution)/shard_map/c...kq,cdqm->d...km/dot_general | solution.py:36
  146.1 17.6 %multiply_subtract_fusion.1 = (f32[1,1024,32,128]{1,3,2,0:T(8,128)S(1)}, f32[1,1024,32,128]{1,3,2,0:T(8,128)}) fusion(f32[2,1024,32,128]{1,3,2,0:T(8,128)} %fusion.7, f32[32,128]{1,0:T(8,128)S(1)} %copy.78, f32[32,128]{1,0:T(8,128)S(1)} %copy.77), kind=kLoop, calls=%fused_computation.27 | loop fusion | flops 25165824 | bytes 67141632 | tf_op jit(solution)/shard_map/sub | solution.py:49
  163.7 34.3 %fusion.10 = f32[2,1024,32,128]{1,3,2,0:T(8,128)} fusion(f32[1,1024,32,128]{1,3,2,0:T(8,128)} %get-tuple-element.25, f32[1,1024,32,128]{1,3,2,0:T(8,128)S(1)} %get-tuple-element.24, f32[1,2,128,128]{2,3,1,0:T(8,128)S(1)} %get-tuple-element.47, f32[1,2,128,128]{2,3,1,0:T(8,128)S(1)} %get-tuple-element.46), kind=kOutput, calls=%fused_computation.21 | convolution fusion | flops 25778257920 | bytes 67371008 | tf_op jit(solution)/shard_map/c...kq,cdqn->d...kn/dot_general | solution.py:36
  198.0 17.6 %multiply_subtract_fusion = (f32[1,1024,32,128]{1,3,2,0:T(8,128)S(1)}, f32[1,1024,32,128]{1,3,2,0:T(8,128)}) fusion(f32[2,1024,32,128]{1,3,2,0:T(8,128)} %fusion.10, f32[32,128]{1,0:T(8,128)S(1)} %get-tuple-element.78, f32[32,128]{1,0:T(8,128)S(1)} %get-tuple-element.79), kind=kLoop, calls=%fused_computation.25 | loop fusion | flops 25165824 | bytes 67141632 | tf_op jit(solution)/shard_map/sub | solution.py:49
  215.6 18.7 %pad_maximum_fusion.1 = f32[2,1024,32,128]{1,3,2,0:T(8,128)} fusion(f32[1,1024,32,128]{1,3,2,0:T(8,128)} %get-tuple-element.23, f32[1,1024,32,128]{1,3,2,0:T(8,128)S(1)} %get-tuple-element.22), kind=kLoop, calls=%fused_computation.11 | loop fusion | flops 8388608 | bytes 67108864 | tf_op jit(solution)/shard_map/stack | solution.py:47
  234.3 33.9 %copy.81 = f32[2,1024,32,128]{3,2,0,1:T(8,128)} copy(f32[2,1024,32,128]{1,3,2,0:T(8,128)} %pad_maximum_fusion.1) | data formatting | bytes 67108864 | tf_op jit(solution)/shard_map/stack | solution.py:47
  268.3 22.3 %fusion.33 = f32[2,3,128,1024]{2,1,3,0:T(4,128)} fusion(f32[2,1024,32,128]{3,2,0,1:T(8,128)} %copy.81, f32[1,2,32,3]{2,3,0,1:T(4,128)S(1)} %get-tuple-element.55, f32[1,2,32,3]{2,3,0,1:T(4,128)S(1)} %get-tuple-element.54), kind=kOutput, calls=%fused_computation.71 | convolution fusion | flops 603980160 | bytes 36701696 | tf_op jit(solution)/shard_map/clkn,cdkm->dmnl/dot_general | solution.py:36
  290.5 3.8 copy.82
  295.3 4.1 copy.83
  299.3 5.3 %all-to-all-start = ((f32[2,384,1024]{2,0,1:T(2,128)}), f32[2,384,1024]{2,0,1:T(2,128)S(1)}, u32[]{:S(2)}, u32[]{:S(2)}) async-start(f32[2,384,1024]{2,0,1:T(2,128)} %copy.83), calls=%async_computation | async-start | bytes 6291456 | tf_op jit(solution)/shard_map/all_to_all | solution.py:90
  304.7 1.9 reshape.443
  306.5 1.9 slice_bitcast_fusion.7
  311.4 1.5 copy.107
  312.9 1.5 copy.110
  316.0 1.5 copy.92
  317.5 1.5 copy.95
  319.0 1.5 copy.98
  328.5 43.6 %all-to-all-done = f32[2,384,1024]{2,0,1:T(2,128)S(1)} async-done(((f32[2,384,1024]{2,0,1:T(2,128)}), f32[2,384,1024]{2,0,1:T(2,128)S(1)}, u32[]{:S(2)}, u32[]{:S(2)}) %all-to-all-start) | async-done | bytes 3145760 | tf_op jit(solution)/shard_map/all_to_all | solution.py:90
  373.1 3.7 copy.85
  376.7 3.5 reshape.556
  380.3 3.7 convolution_bitcast_fusion.1
  385.4 5.2 fusion.40
  390.8 5.2 collective-permute-start
  396.8 11.7 %collective-permute-done = f32[2,19,32,128]{3,2,1,0:T(8,128)S(1)} collective-permute-done((f32[2,19,32,128]{3,2,1,0:T(8,128)S(1)}, f32[2,19,32,128]{3,2,1,0:T(8,128)S(1)}, u32[]{:S(2)}, u32[]{:S(2)}) %collective-permute-start) | collective-permute-done | bytes 622624 | tf_op jit(solution)/shard_map/ppermute | solution.py:17
  409.2 2.6 copy.90
  411.7 2.9 gather_fusion.3
  414.7 4.6 gather_fusion.4
  419.3 4.7 gather_fusion.5
  424.0 4.7 gather_fusion.6
  428.7 4.5 gather_fusion.7
  433.2 4.6 gather_fusion.8
  437.8 4.6 gather_fusion.2
  442.5 4.7 gather_fusion.1
  447.2 28.9 %fusion.22 = f32[2,96,32,128]{3,1,0,2:T(8,128)S(1)} fusion(f32[96,2,32,128]{3,2,1,0:T(8,128)} %gather_fusion.8, f32[96,2,32,128]{3,2,1,0:T(8,128)} %gather_fusion.7, f32[96,2,32,128]{3,2,1,0:T(8,128)} %gather_fusion.6, f32[96,2,32,128]{3,2,1,0:T(8,128)} %gather_fusion.5, f32[96,2,32,128]{3,2,1,0:T(8,128)} %gather_fusion.4, ...), kind=kLoop, calls=%fused_computation.44 | loop fusion | flops 18087936 | bytes 28443392 | tf_op jit(solution)/shard_map/add | solution.py:102
  476.1 6.1 %multiply_subtract_fusion.4 = (f32[1,96,32,128]{3,1,0,2:T(8,128)S(1)}, f32[1,96,32,128]{3,1,0,2:T(8,128)S(1)}) fusion(f32[2,96,32,128]{3,1,0,2:T(8,128)S(1)} %fusion.22, f32[32,128]{1,0:T(8,128)S(1)} %copy-done.15, f32[96]{0:T(128)S(1)} %bitcast.270), kind=kLoop, calls=%fused_computation.79 | loop fusion | flops 3538944 | bytes 6308224 | tf_op jit(solution)/shard_map/sub | solution.py:49
  482.2 2.9 fusion.39
  485.9 6.1 %fusion.36 = f32[2,96,32,128]{3,2,1,0:T(8,128)} fusion(f32[2,96,32,128]{3,1,2,0:T(8,128)S(1)} %pad_maximum_fusion.4, f32[1,2,32,32]{2,3,1,0:T(8,128)S(1)} %get-tuple-element.51, f32[1,2,32,32]{2,3,1,0:T(8,128)S(1)} %get-tuple-element.50), kind=kOutput, calls=%fused_computation.72 | convolution fusion | flops 603983872 | bytes 6307840 | tf_op jit(solution)/shard_map/c...kn,cdkm->d...mn/dot_general | solution.py:36
  492.0 2.9 reshape.447
  495.1 1.9 collective-permute-start.1
  497.0 3.0 fusion.85
  500.1 2.2 collective-permute-done.1
  502.4 1.8 gather_fusion
  505.3 3.3 fusion.19
  508.6 11.4 %psum.7 = f32[]{:T(128)} all-reduce(f32[]{:T(128)} %fusion.19), channel_id=1, replica_groups=mesh['chip'=8,'line'=4] {'line'}, use_global_device_ids=true, to_apply=%region_1.3 | all-reduce | flops 1 | bytes 8 | tf_op jit(solution)/shard_map/psum | solution.py:124
  (106 shorter events, 24.1 us)
Async XLA Ops:
  0.3 41.3 %copy-start.7 = (f32[32,128]{1,0:T(8,128)}, f32[32,128]{1,0:T(8,128)S(1)}, u32[]{:S(2)}) copy-start(f32[32,128]{1,0:T(8,128)S(1)} %get-tuple-element.72) | copy-start | bytes 49156
  0.3 41.3 %copy-start.9 = (f32[32,128]{1,0:T(8,128)}, f32[32,128]{1,0:T(8,128)S(1)}, u32[]{:S(2)}) copy-start(f32[32,128]{1,0:T(8,128)S(1)} %get-tuple-element.73) | copy-start | bytes 49156
  1.5 196.5 %copy-start.5 = (f32[32,128]{1,0:T(8,128)}, f32[32,128]{1,0:T(8,128)S(1)}, u32[]{:S(2)}) copy-start(f32[32,128]{1,0:T(8,128)S(1)} %get-tuple-element.79) | copy-start | bytes 49156
  3.3 15.1 %copy-start.16 = (f32[2,4096]{1,0:T(2,128)S(1)}, f32[2,4096]{1,0:T(2,128)}, u32[]{:S(2)}) copy-start(f32[2,4096]{1,0:T(2,128)} %param.10) | copy-start | bytes 98308
  18.9 22.6 %copy-start.3 = (f32[1,2,32,32]{2,3,0,1:T(8,128)}, f32[1,2,32,32]{2,3,0,1:T(8,128)S(1)}, u32[]{:S(2)}) copy-start(f32[1,2,32,32]{2,3,0,1:T(8,128)S(1)} %get-tuple-element.52) | copy-start | bytes 24580
  18.9 22.6 %copy-start.4 = (f32[1,2,32,32]{2,3,0,1:T(8,128)}, f32[1,2,32,32]{2,3,0,1:T(8,128)S(1)}, u32[]{:S(2)}) copy-start(f32[1,2,32,32]{2,3,0,1:T(8,128)S(1)} %get-tuple-element.53) | copy-start | bytes 24580
  78.2 0.7 copy-start.1
  234.3 33.9 %copy-start.17 = (f32[1,32,3]{1,2,0:T(4,128)S(1)}, f32[1,32,3]{1,2,0:T(4,128)}, u32[]{:S(2)}) copy-start(f32[1,32,3]{1,2,0:T(4,128)} %get-tuple-element.80) | copy-start | bytes 1156
  234.3 33.9 %copy-start.18 = (f32[1,32,3]{1,2,0:T(4,128)S(1)}, f32[1,32,3]{1,2,0:T(4,128)}, u32[]{:S(2)}) copy-start(f32[1,32,3]{1,2,0:T(4,128)} %get-tuple-element.81) | copy-start | bytes 1156
  234.3 33.9 %copy-start.19 = (f32[1,32,3]{1,2,0:T(4,128)S(1)}, f32[1,32,3]{1,2,0:T(4,128)}, u32[]{:S(2)}) copy-start(f32[1,32,3]{1,2,0:T(4,128)} %fusion.77) | copy-start | bytes 1156
  299.3 72.7 %all-to-all-start = ((f32[2,384,1024]{2,0,1:T(2,128)}), f32[2,384,1024]{2,0,1:T(2,128)S(1)}, u32[]{:S(2)}, u32[]{:S(2)}) async-start(f32[2,384,1024]{2,0,1:T(2,128)} %copy.83), calls=%async_computation | async-start | bytes 6291456 | tf_op jit(solution)/shard_map/all_to_all | solution.py:90
  380.2 3.7 copy-start.8
  380.2 3.7 copy-start.10
  384.5 0.9 copy-start.2
  390.8 17.7 %collective-permute-start = (f32[2,19,32,128]{3,2,1,0:T(8,128)S(1)}, f32[2,19,32,128]{3,2,1,0:T(8,128)S(1)}, u32[]{:S(2)}, u32[]{:S(2)}) collective-permute-start(f32[2,19,32,128]{3,2,1,0:T(8,128)S(1)} %copy.88), channel_id=1, source_target_pairs={{1,0},{2,1},{3,2},{5,4},{6,5},{7,6},{9,8},{10,9},{11,10},{13,12},{... | collective-permute-start | bytes 1867784 | tf_op jit(solution)/shard_map/ppermute | solution.py:17
  442.4 4.7 copy-start.11
  442.4 4.7 copy-start.12
  442.4 4.7 copy-start.13
  442.4 4.7 copy-start.14
  447.2 28.9 %copy-start.15 = (f32[32,128]{1,0:T(8,128)S(1)}, f32[32,128]{1,0:T(8,128)}, u32[]{:S(2)}) copy-start(f32[32,128]{1,0:T(8,128)} %fusion.63) | copy-start | bytes 49156
  447.2 28.9 %copy-start.22 = (f32[1,96]{1,0:T(1,128)S(1)}, f32[1,96]{1,0:T(1,128)}, u32[]{:S(2)}) copy-start(f32[1,96]{1,0:T(1,128)} %param.12) | copy-start | bytes 1156
  482.2 2.9 copy-start.6
  495.1 9.1 %copy-start.20 = (pred[128]{0:T(512)(128)(4,1)S(1)}, pred[128]{0:T(512)(128)(4,1)}, u32[]{:S(2)}) copy-start(pred[128]{0:T(512)(128)(4,1)} %get-tuple-element.92) | copy-start | bytes 388
  495.1 9.1 %copy-start.21 = (pred[128]{0:T(512)(128)(4,1)S(1)}, pred[128]{0:T(512)(128)(4,1)}, u32[]{:S(2)}) copy-start(pred[128]{0:T(512)(128)(4,1)} %get-tuple-element.93) | copy-start | bytes 388
  495.1 9.1 %copy-start.23 = (f32[128]{0:T(128)S(1)}, f32[128]{0:T(128)}, u32[]{:S(2)}) copy-start(f32[128]{0:T(128)} %get-tuple-element.90) | copy-start | bytes 1540
  495.1 9.1 %copy-start.24 = (f32[128]{0:T(128)S(1)}, f32[128]{0:T(128)}, u32[]{:S(2)}) copy-start(f32[128]{0:T(128)} %get-tuple-element.91) | copy-start | bytes 1540
  495.1 7.3 %collective-permute-start.1 = (f32[2,96,128]{1,0,2:T(2,128)S(1)}, f32[2,96,128]{1,0,2:T(2,128)}, u32[]{:S(2)}, u32[]{:S(2)}) collective-permute-start(f32[2,96,128]{1,0,2:T(2,128)S(1)} %copy.146), channel_id=1, source_target_pairs={{0,4},{4,8},{8,12},{12,16},{16,20},{20,24},{24,28},{1,5},{5,9},{9,... | collective-permute-start | bytes 294920 | tf_op jit(solution)/shard_map/ppermute | solution.py:17
  500.0 20.7 %copy-start = (f32[1,2,96,3968]{3,2,1,0:T(8,128)S(1)}, f32[1,2,96,3968]{3,2,1,0:T(8,128)}, u32[]{:S(2)}) copy-start(f32[1,2,96,3968]{3,2,1,0:T(8,128)} %get-tuple-element.35) | copy-start | bytes 9142276
where the time goes:
time: 532 us; the launch traced here: 522 us
  matrix products  164 us (31%)
  other arithmetic  145 us (27%)
  local copies, waits for them, and re-layouts  129 us (24%)
  waiting for transfers between devices  57.5 us (11%)
  starting transfers between devices  12.4 us (2%)
  blocking collectives  11.4 us (2%)
    dot_general x8, matrix products, complex_einsum(): jnp.einsum(form, pair, stacked_table(table), precision=lax.Precision.HIGH...  164 us
    sub x6, other arithmetic, complex_scale(): pair[0] * factor_real - pair[1] * factor_imag  60.4 us
    all_to_all x1, waiting for transfers between devices, local(): lax.all_to_all(compressed, 'line', split_axis=1, concat_axis=2, tiled=True)  43.6 us
    another operation x4, other arithmetic, complex_scale(): jnp.stack([pair[0] * factor_real - pair[1] * factor_imag, pair[0] * facto...  37.9 us
    gather x8, local copies, waits for them, and re-layouts, local(): picked = jnp.take(extended, positions + offset, axis=1)  35.4 us
    another operation x1, local copies, waits for them, and re-layouts, complex_scale(): jnp.stack([pair[0] * factor_real - pair[1] * factor_imag, pair[0] * facto...  33.9 us
    add x1, other arithmetic, local(): migrated = migrated + weights[offset] * picked  28.9 us
    unnamed x53, local copies, waits for them, and re-layouts  16.7 us
  transfers between devices with their start and end apart: 3, of which 3 were waited for; matrix products, arithmetic and copies ran while one was open for 5% of the time, Pallas kernels for 0%

commit v1 on v0

v1 whole, which is shorter than its diff:
```python
import math

import jax
import jax.numpy as jnp
import numpy as np
from jax import lax
from jax.experimental import pallas as pl
from jax.experimental.pallas import tpu as pltpu
from jax.sharding import PartitionSpec as P


RKEEP = 384
TAPS = 8
MAXSHIFT = 12
LANES = 128
MARGIN = MAXSHIFT + TAPS - 1

F32 = jnp.float32
ANY = pl.BlockSpec(memory_space=pl.ANY)
VMEM = pl.BlockSpec(memory_space=pltpu.VMEM)
BF16 = jnp.bfloat16


def split_np(table):
    high = table.astype(jnp.bfloat16)
    low = (table - high.astype(np.float64)).astype(jnp.bfloat16)
    return high, low


def root(length, index, sign):
    angle = sign * 2.0 * np.pi * (np.asarray(index) % length) / length
    return np.cos(angle), np.sin(angle)


def lane_matrix(sign, scale=1.0):
    index = np.arange(LANES)
    real, imag = root(LANES, np.outer(index, index), sign)
    full = scale * np.block([[real, imag], [-imag, real]])
    high, low = split_np(full)
    return np.concatenate([high, high, low], axis=0)


def column_twiddle(columns, length, sign, scale=1.0):
    real, imag = root(length, np.outer(np.arange(columns), np.arange(LANES)), sign)
    return (scale * np.stack([real, imag])).astype(np.float32)


def cmul_const(value, real, imag):
    vr, vi = value
    near = 1e-12
    if abs(imag) < near:
        if abs(real - 1.0) < near:
            return value
        if abs(real + 1.0) < near:
            return (-vr, -vi)
    if abs(real) < near:
        if imag > 0:
            return (-vi, vr)
        return (vi, -vr)
    if abs(abs(real) - abs(imag)) < near:
        mag = abs(real)
        sr, si = (1.0 if real > 0 else -1.0), (1.0 if imag > 0 else -1.0)
        if sr == si:
            return ((vr - vi) * (mag * sr), (vr + vi) * (mag * sr))
        return ((vr + vi) * (mag * sr), (vi - vr) * (mag * sr))
    return (vr * real - vi * imag, vr * imag + vi * real)


def cadd(a, b):
    return (a[0] + b[0], a[1] + b[1])


def csub(a, b):
    return (a[0] - b[0], a[1] - b[1])


def dft_list(values, sign):
    count = len(values)
    if count == 1:
        return values
    if count == 2:
        return [cadd(values[0], values[1]), csub(values[0], values[1])]
    if count == 4:
        even = [cadd(values[0], values[2]), csub(values[0], values[2])]
        odd = [cadd(values[1], values[3]), csub(values[1], values[3])]
        turn = cmul_const(odd[1], 0.0, float(sign))
        return [cadd(even[0], odd[0]), cadd(even[1], turn), csub(even[0], odd[0]), csub(even[1], turn)]
    even = dft_list(values[0::2], sign)
    odd = dft_list(values[1::2], sign)
    low, high = [], []
    for k in range(count // 2):
        real, imag = root(count, k, sign)
        turned = cmul_const(odd[k], float(real), float(imag))
        low.append(cadd(even[k], turned))
        high.append(csub(even[k], turned))
    return low + high


def split3(value):
    high = value.astype(BF16)
    low = (value - high.astype(F32)).astype(BF16)
    return high, low


def dot_nn(a, b):
    return lax.dot_general(a, b, (((1,), (0,)), ((), ())), preferred_element_type=F32)


def dot_nt(a, b):
    return lax.dot_general(a, b, (((1,), (1,)), ((), ())), preferred_element_type=F32)


def response_tables(length):
    columns = length // LANES
    group = LANES // columns
    index = np.arange(LANES)
    firsts = []
    for b in range(group):
        real, imag = root(LANES, np.outer(index, np.arange(columns) * group + b), -1)
        firsts.append(np.block([[real, -imag], [imag, real]]))
    first = np.concatenate(firsts, axis=1).astype(np.float32)
    tw = column_twiddle(columns, length, -1, 1.0 / length).reshape(2 * columns, LANES)
    real, imag = root(columns, np.outer(np.arange(columns), np.arange(columns)), -1)
    last = np.block([[real, -imag], [imag, real]]).astype(np.float32)
    table = np.zeros((2 * LANES + 2 * columns, max(2 * LANES, LANES + 2 * columns)), np.float32)
    table[:2 * LANES, :2 * LANES] = first
    table[2 * LANES:, :LANES] = tw
    table[2 * LANES:, LANES:LANES + 2 * columns] = last
    return table


def response(f_ref, table_ref, out_ref):
    columns = out_ref.shape[1]
    group = LANES // columns
    parts = []
    for c in range(2):
        parts.append(jnp.concatenate(
            [f_ref[c:c + 1, j * LANES:(j + 1) * LANES] for j in range(columns)], axis=0))
    blocks = []
    for b in range(group):
        sl = slice(columns * b, columns * (b + 1))
        blocks.append(jnp.concatenate([parts[0][:, sl], parts[1][:, sl]], axis=0))
    rhs = jnp.concatenate(blocks, axis=0)
    half = lax.dot_general(
        table_ref[:2 * LANES, :2 * LANES], rhs, (((1,), (0,)), ((), ())),
        precision=lax.Precision.HIGHEST, preferred_element_type=F32)
    re = half[:LANES].T
    im = half[LANES:].T
    twr = table_ref[2 * LANES:2 * LANES + columns, :LANES]
    twi = table_ref[2 * LANES + columns:2 * LANES + 2 * columns, :LANES]
    pair = jnp.concatenate([re * twr - im * twi, re * twi + im * twr], axis=0)
    full = lax.dot_general(
        table_ref[2 * LANES:, LANES:LANES + 2 * columns], pair, (((1,), (0,)), ((), ())),
        precision=lax.Precision.HIGHEST, preferred_element_type=F32)
    out_ref[0] = full[:columns]
    out_ref[1] = full[columns:]


def toeplitz(g_ref, table, count, per, start, rows, columns):
    base = [
        jnp.concatenate([jnp.broadcast_to(g_ref[c, j:j + 1, :], (8, LANES)) for j in range(columns)], axis=1)
        for c in range(2)
    ]
    base = [pltpu.roll(b, 0, 1, stride=1, stride_axis=0) for b in base]
    sub = lax.broadcasted_iota(jnp.int32, (8, LANES), 0)
    half = count * rows
    group = 16 if half % 16 == 0 else 8
    order = [per * d + start + r8 for d in range(count) for r8 in range(0, rows, 8)]
    for at in range(0, half, group):
        pieces = [[], []]
        for shift in order[at // 8:(at + group) // 8]:
            bins = (sub + shift).astype(F32)
            gain = 1.0 + 2.0 * bins / RKEEP
            gain = jnp.concatenate([gain] * columns, axis=1)
            for c in range(2):
                pieces[c].append(pltpu.roll(base[c], shift % (columns * LANES), 1) * gain)
        grh, grl = split3(jnp.concatenate(pieces[0], axis=0))
        gih, gil = split3(jnp.concatenate(pieces[1], axis=0))
        for n, (plain, crossed) in enumerate(((grh, -gih), (gih, grh), (grl, -gil), (gil, grl))):
            table[0, n * half + at:n * half + at + group, :] = plain
            table[1, n * half + at:n * half + at + group, :] = crossed


def scatter(me_ref, outs, turned):
    count = len(outs)
    for s in range(count):
        dest = lax.rem(me_ref[0] + s, count)
        outs[s][0] = turned[0, dest]
        outs[s][1] = turned[1, dest]


def turn(acc, turned, at):
    width = acc.shape[1] // 2
    both = acc[:, :width] + acc[:, width:]
    turned[:, :, :, pl.ds(at, acc.shape[0])] = both.T.reshape(turned.shape[:3] + (acc.shape[0],))


def compress_first(echoes, range_filter, me, count, per, rows):
    lines, samples = echoes.shape[2], echoes.shape[3]
    columns = samples // LANES
    blocks = max(1, min(4, samples // 1024))
    kblk = samples // blocks
    width = 2 * count * rows
    mblk = min(512, lines)
    tables = response_tables(samples)

    def kernel(me_ref, x_hbm, f_hbm, t_hbm, *refs):
        outs, refs = refs[:count], refs[count:]
        g_ref, x_ref, f_ref, t_ref, table, acc, turned, sems = refs
        small = [pltpu.make_async_copy(f_hbm, f_ref, sems.at[2 * blocks]),
                 pltpu.make_async_copy(t_hbm, t_ref, sems.at[2 * blocks + 1])]
        large = []
        for k in range(blocks):
            for c in range(2):
                ks = slice(k * kblk, (k + 1) * kblk)
                large.append(pltpu.make_async_copy(
                    x_hbm.at[0, c, :, ks], x_ref.at[c, :, ks], sems.at[2 * k + c]))
        for copy in small + large:
            copy.start()
        for copy in small:
            copy.wait()
        response(f_ref, t_ref, g_ref)
        toeplitz(g_ref, table, count, per, 0, rows, columns)
        for k in range(blocks):
            ks = slice(k * kblk, (k + 1) * kblk)
            large[2 * k].wait()
            large[2 * k + 1].wait()

            def body(m, carry):
                at = pl.multiple_of(m * mblk, mblk)
                ms = pl.ds(at, mblk)
                part = dot_nt(x_ref[0, ms, ks], table[0, :, ks]) + dot_nt(x_ref[1, ms, ks], table[1, :, ks])
                if k > 0:
                    part = part + acc[ms, :]
                if k < blocks - 1:
                    acc[ms, :] = part
                else:
                    turn(part, turned, at)
                return carry

            lax.fori_loop(0, lines // mblk, body, 0)
        scatter(me_ref, outs, turned)

    hbm = pl.BlockSpec(memory_space=pltpu.HBM)
    out = jax.ShapeDtypeStruct((2, rows, lines), F32)
    results = pl.pallas_call(
        kernel,
        in_specs=[pl.BlockSpec(memory_space=pltpu.SMEM), hbm, hbm, hbm],
        out_specs=[VMEM] * (count + 2),
        out_shape=[out] * count + [
            jax.ShapeDtypeStruct((2, columns, LANES), F32),
            jax.ShapeDtypeStruct((2, lines, samples), BF16)],
        scratch_shapes=[
            pltpu.VMEM(range_filter.shape, F32),
            pltpu.VMEM(tables.shape, F32),
            pltpu.VMEM((2, 2 * width, samples), BF16),
            pltpu.VMEM((lines, 2 * width), F32),
            pltpu.VMEM((2, count, rows, lines), F32),
            pltpu.SemaphoreType.DMA((2 * blocks + 2,)),
        ],
        compiler_params=pltpu.CompilerParams(vmem_limit_bytes=(26 if rows * count <= 64 else 48) * 2**20),
        cost_estimate=pl.CostEstimate(
            flops=8 * lines * samples * 2 * width, bytes_accessed=4 * lines * samples, transcendentals=0),
        name="compress",
    )(me, echoes, range_filter, tables)
    return results[:count], results[count], results[count + 1]


def compress(x, g, me, count, per, start, rows, after):
    lines, samples = x.shape[1], x.shape[2]
    columns = samples // LANES
    width = 2 * count * rows
    mblk = min(256, lines)

    def kernel(me_ref, x_ref, g_ref, _, *refs):
        outs = refs[:count]
        table, turned = refs[count:]
        toeplitz(g_ref, table, count, per, start, rows, columns)

        def body(m, carry):
            at = pl.multiple_of(m * mblk, mblk)
            ms = pl.ds(at, mblk)
            turn(dot_nt(x_ref[0, ms, :], table[0]) + dot_nt(x_ref[1, ms, :], table[1]), turned, at)
            return carry

        lax.fori_loop(0, lines // mblk, body, 0)
        scatter(me_ref, outs, turned)

    return pl.pallas_call(
        kernel,
        in_specs=[pl.BlockSpec(memory_space=pltpu.SMEM), VMEM, VMEM, ANY],
        out_specs=[VMEM] * count,
        out_shape=[jax.ShapeDtypeStruct((2, rows, lines), F32)] * count,
        scratch_shapes=[
            pltpu.VMEM((2, 2 * width, samples), BF16),
            pltpu.VMEM((2, count, rows, lines), F32),
        ],
        compiler_params=pltpu.CompilerParams(vmem_limit_bytes=(6 + rows * count // 10) * 2**20),
        cost_estimate=pl.CostEstimate(
            flops=8 * lines * samples * 2 * width, bytes_accessed=4 * lines * samples, transcendentals=0),
        name="compress",
    )(me, x, g, after)


def doppler(chunks, tw, matrix, lead, after):
    count = len(chunks[0])
    lines = chunks[0][0].shape[2]
    sizes = [pieces[0].shape[1] for pieces in chunks]
    rows = sum(sizes)
    own = lines // LANES
    columns = own * count
    number = count * len(chunks)

    def kernel(*refs):
        tw_ref, mat_ref = refs[number:number + 2]
        outs, scratch = refs[number + 2 + len(after):-1], refs[-1]
        out_ref = outs[0]
        begun = 0
        for n, size in enumerate(sizes):
            ins = refs[n * count:(n + 1) * count]
            for r8 in range(0, size, 8):
                rs = slice(r8, r8 + 8)
                inner = [[None] * own for _ in range(count)]
                for p in range(own):
                    ls = slice(p * LANES, (p + 1) * LANES)
                    spread = dft_list([(ref[0, rs, ls], ref[1, rs, ls]) for ref in ins], 1)
                    for k0 in range(count):
                        real, imag = root(columns, p * k0, -1)
                        inner[k0][p] = cmul_const(spread[k0], float(real), float(imag))
                for k0 in range(count):
                    for k1, (vr, vi) in enumerate(dft_list(inner[k0], -1)):
                        k = k0 + count * k1
                        tr = tw_ref[0, k:k + 1, :]
                        ti = tw_ref[1, k:k + 1, :]
                        at = k * rows + begun + r8
                        scratch[at:at + 8, :LANES] = vr * tr - vi * ti
                        scratch[at:at + 8, LANES:] = vr * ti + vi * tr
            begun += size
        high, low = split3(scratch[...])
        out = dot_nn(jnp.concatenate([high, low, high], axis=1), mat_ref[...])
        out_ref[0] = out[:, :LANES].reshape(columns, rows, LANES)
        out_ref[1] = out[:, LANES:].reshape(columns, rows, LANES)
        if lead:
            for c in range(2):
                for k in range(columns):
                    at = (c * columns + k) * lead
                    outs[1][at:at + lead, :] = out_ref[c, k, :lead, :]

    return pl.pallas_call(
        kernel,
        in_specs=[VMEM] * (number + 2) + [ANY] * len(after),
        out_shape=[jax.ShapeDtypeStruct((2, columns, rows, LANES), F32)]
        + ([jax.ShapeDtypeStruct((2 * columns * lead, LANES), F32)] if lead else []),
        compiler_params=pltpu.CompilerParams(vmem_limit_bytes=16 * 2**20),
        scratch_shapes=[pltpu.VMEM((columns * rows, 2 * LANES), F32)],
        cost_estimate=pl.CostEstimate(
            flops=2 * columns * rows * 256 * 768, bytes_accessed=16 * columns * rows * LANES, transcendentals=0),
        name="doppler",
    )(*[piece for pieces in chunks for piece in pieces], tw, matrix, *after)


def turn_pair(turns):
    folds = jnp.floor(2.0 * turns + 0.5)
    rest = turns - 0.5 * folds
    sign = 1.0 - 2.0 * (folds - 2.0 * jnp.floor(0.5 * folds))
    z = rest * rest
    cos_c = [(-1) ** j * (2 * math.pi) ** (2 * j) / math.factorial(2 * j) for j in range(7)]
    sin_c = [(-1) ** j * (2 * math.pi) ** (2 * j + 1) / math.factorial(2 * j + 1) for j in range(7)]
    c = cos_c[-1] * z + cos_c[-2]
    s = sin_c[-1] * z + sin_c[-2]
    for j in range(4, -1, -1):
        c = c * z + cos_c[j]
        s = s * z + sin_c[j]
    return c * sign, s * (rest * sign)


def phases(fm, weights, columns, splits):
    pick = np.zeros((LANES, LANES), np.float32)
    width = LANES // columns
    for b in range(width):
        for p in range(columns):
            pick[b * columns + p, width * p + b] = 1.0
    per = fm.shape[0]
    length = columns * LANES
    coarse = 2048
    together = 8

    def kernel(fm_ref, w_ref, pick_ref, *outs):
        outs, w_out = outs[:-1], outs[-1]

        @pl.when(pl.program_id(0) == 0)
        def _():
            rows_in = []
            for t in range(TAPS):
                tap = jnp.concatenate(
                    [w_ref[t:t + 1, p * LANES:(p + 1) * LANES] for p in range(columns)], axis=0).T
                rows_in.append(jnp.concatenate(
                    [tap[b * columns:(b + 1) * columns, :] for b in range(width)], axis=1))
            w_out[...] = lax.dot_general(
                jnp.concatenate(rows_in, axis=0), pick_ref[...], (((1,), (0,)), ((), ())),
                precision=lax.Precision.HIGHEST, preferred_element_type=F32)

        for i in range(together):
            k = pl.program_id(0) * together + i
            lane = lax.broadcasted_iota(jnp.int32, (1, LANES), 1)
            index = k + columns * lane
            index = jnp.where(index >= length // 2, index - length, index)
            square = index * index
            upper = (square // coarse).astype(F32)
            lower = (square % coarse).astype(F32)
            scale = 1.0 / (2.0 * length * length)
            first = 0
            for out, rows in zip(outs, splits):
                rate = fm_ref[first:first + rows, :]
                whole = jnp.floor(rate)
                part = rate - whole
                turns = whole * (upper * (coarse * scale))
                turns = turns - jnp.floor(turns)
                turns = turns + whole * (lower * scale) + part * (square.astype(F32) * scale)
                c, s = turn_pair(turns)
                out[0, i] = c
                out[1, i] = -s
                first += rows

    return pl.pallas_call(
        kernel,
        grid=(columns // together,),
        in_specs=[pl.BlockSpec(a, lambda k: (0, 0)) for a in ((per, LANES), weights.shape, pick.shape)],
        out_specs=[pl.BlockSpec((2, together, rows, LANES), lambda k: (0, k, 0, 0)) for rows in splits]
        + [pl.BlockSpec((TAPS * columns, LANES), lambda k: (0, 0))],
        out_shape=[jax.ShapeDtypeStruct((2, columns, rows, LANES), F32) for rows in splits]
        + [jax.ShapeDtypeStruct((TAPS * columns, LANES), F32)],
        cost_estimate=pl.CostEstimate(
            flops=60 * columns * per * LANES, bytes_accessed=8 * columns * per * LANES, transcendentals=0),
        compiler_params=pltpu.CompilerParams(vmem_limit_bytes=8 * 2**20),
        name="phases",
    )(jnp.broadcast_to(fm[:, None], (per, LANES)), weights, pick)


def focus_rows(parts, weights, shift, phase, tw, matrix, first, rows, earlier):
    columns = phase.shape[1]
    total = sum(take for _, _, take in parts)
    reach = -(-(rows + MAXSHIFT) // 8) * 8
    pitch_d = max(total, reach + 8)
    pitch_d += 1 - pitch_d % 2
    pitch_u = reach + 1
    pitch_m = rows + 1

    def kernel(shift_ref, *refs):
        ins = refs[:len(parts)]
        w_ref, ph_ref, tw_ref, mat_ref = refs[len(parts):len(parts) + 4]
        before = refs[len(parts) + 4:len(parts) + 4 + len(earlier)]
        out_ref, head_ref, tail_ref, en_ref, dop, sums, moved, scratch = refs[len(parts) + 4 + len(earlier):]
        base = 0
        for ref in before:
            tail_ref[:, base:base + ref.shape[1], :] = ref[...]
            base += ref.shape[1]

        def combine(k, carry):
            taps = [w_ref[pl.ds(t * columns + k, 1), :] for t in range(TAPS)]
            for c in range(2):
                at = (c * columns + k) * pitch_d
                filled = 0
                for ref, (a, begin, take) in zip(ins, parts):
                    if len(a.shape) == 4:
                        piece = ref[c, k, begin:begin + take, :]
                    else:
                        piece = ref[pl.ds((c * columns + k) * take, take), :]
                    dop[pl.ds(at + filled, take), :] = piece
                    filled += take
                if filled < reach + 8:
                    dop[pl.ds(at + filled, reach + 8 - filled), :] = jnp.zeros((reach + 8 - filled, LANES), F32)
                to = (c * columns + k) * pitch_u
                for r8 in range(0, reach, 8):
                    value = taps[0] * dop[pl.ds(at + r8, 8), :]
                    for t in range(1, TAPS):
                        value = value + taps[t] * dop[pl.ds(at + r8 + t, 8), :]
                    sums[pl.ds(to + r8, 8), :] = value
            return carry

        lax.fori_loop(0, columns, combine, 0)

        def move(r, carry):
            source = r + shift_ref[first + r]
            for c in range(2):
                for k8 in range(0, columns, 8):
                    lead = c * columns + k8
                    moved[pl.ds(lead * pitch_m + r, 8, stride=pitch_m), :] = (
                        sums[pl.ds(lead * pitch_u + source, 8, stride=pitch_u), :])
            return carry

        lax.fori_loop(0, rows, move, 0)

        for k in range(columns):
            at = slice(k * rows, (k + 1) * rows)
            vr = moved[k * pitch_m:k * pitch_m + rows, :]
            vi = moved[(columns + k) * pitch_m:(columns + k) * pitch_m + rows, :]
            pr, pi = ph_ref[0, k], ph_ref[1, k]
            scratch[at, :LANES] = vr * pr - vi * pi
            scratch[at, LANES:] = vr * pi + vi * pr
        high, low = split3(scratch[...])
        scratch[...] = dot_nn(jnp.concatenate([high, low, high], axis=1), mat_ref[...])
        total_energy = jnp.zeros((8, LANES), F32)
        for r8 in range(0, rows, 8):
            values = []
            for k in range(columns):
                at = slice(k * rows + r8, k * rows + r8 + 8)
                vr, vi = scratch[at, :LANES], scratch[at, LANES:]
                tr, ti = tw_ref[0, k:k + 1, :], tw_ref[1, k:k + 1, :]
                values.append((vr * tr - vi * ti, vr * ti + vi * tr))
            for j, (vr, vi) in enumerate(dft_list(values, 1)):
                ls = slice(j * LANES, (j + 1) * LANES)
                if j == 0:
                    head_ref[0, r8:r8 + 8, :] = vr
                    head_ref[1, r8:r8 + 8, :] = vi
                else:
                    out_ref[0, r8:r8 + 8, ls] = vr
                    out_ref[1, r8:r8 + 8, ls] = vi
                if j == columns - 1:
                    tail_ref[0, base + r8:base + r8 + 8, :] = vr
                    tail_ref[1, base + r8:base + r8 + 8, :] = vi
                if j > 0:
                    total_energy = total_energy + vr * vr + vi * vi
        en_ref[...] = total_energy

    return pl.pallas_call(
        kernel,
        in_specs=[pl.BlockSpec(memory_space=pltpu.SMEM)] + [VMEM] * (len(parts) + 4 + len(earlier)),
        out_shape=[
            jax.ShapeDtypeStruct((2, rows, columns * LANES), F32),
            jax.ShapeDtypeStruct((2, rows, LANES), F32),
            jax.ShapeDtypeStruct((2, rows + sum(a.shape[1] for a in earlier), LANES), F32),
            jax.ShapeDtypeStruct((8, LANES), F32),
        ],
        scratch_shapes=[
            pltpu.VMEM((-(-2 * columns * pitch_d // 8) * 8 + 8, LANES), F32),
            pltpu.VMEM((-(-2 * columns * pitch_u // 8) * 8 + 8, LANES), F32),
            pltpu.VMEM((-(-2 * columns * pitch_m // 8) * 8 + 8, LANES), F32),
            pltpu.VMEM((columns * rows, 2 * LANES), F32),
        ],
        compiler_params=pltpu.CompilerParams(vmem_limit_bytes=(16 if rows < 32 else 30) * 2**20),
        cost_estimate=pl.CostEstimate(
            flops=2 * columns * rows * 256 * 768, bytes_accessed=32 * columns * rows * LANES, transcendentals=0),
        name="focus",
    )(shift, *[a for a, _, _ in parts], weights, phase, tw, matrix, *earlier)


def blend(heads, earlier, energies, seam):
    number = len(heads)

    def kernel(seam_ref, *refs):
        head_refs, tail_ref, energy_refs = refs[:number], refs[number], refs[number + 1:-number - 1]
        outs, total_ref = refs[-number - 1:-1], refs[-1]
        width, linked = seam_ref[0], seam_ref[1]
        total = energy_refs[0][...]
        for ref in energy_refs[1:]:
            total = total + ref[...]
        first = 0
        for head, out in zip(head_refs, outs):
            rows = head.shape[1]
            for c in range(2):
                now = head[c]
                offsets = lax.broadcasted_iota(jnp.int32, now.shape, 1)
                ramp = (offsets.astype(F32) + 0.5) / width.astype(F32)
                inside = (offsets < width) & (linked == 1)
                before = pltpu.roll(tail_ref[c, first:first + rows, :], width, 1)
                mixed = jnp.where(inside, (1.0 - ramp) * before + ramp * now, now)
                out[c] = mixed
                power = mixed * mixed
                for r8 in range(0, rows, 8):
                    total = total + power[r8:r8 + 8]
            first += rows
        total_ref[...] = total

    return pl.pallas_call(
        kernel,
        in_specs=[pl.BlockSpec(memory_space=pltpu.SMEM)] + [VMEM] * (number + 1 + len(energies)),
        out_shape=[jax.ShapeDtypeStruct(h.shape, F32) for h in heads] + [jax.ShapeDtypeStruct((8, LANES), F32)],
        compiler_params=pltpu.CompilerParams(vmem_limit_bytes=4 * 2**20),
        name="blend",
    )(seam, *heads, earlier, *energies)


def finish(images, heads, energies, pixels):
    number, count = len(images), len(energies)
    total_rows = sum(a.shape[1] for a in images)
    length = images[0].shape[2]

    def kernel(*refs):
        image_refs, head_refs = refs[:number], refs[number:2 * number]
        energy_refs, out_ref = refs[2 * number:-1], refs[-1]
        total = energy_refs[0][...]
        for ref in energy_refs[1:]:
            total = total + ref[...]
        energy = jnp.sum(jnp.sum(total, axis=0, keepdims=True), axis=1, keepdims=True)
        scale = lax.rsqrt(energy / pixels + 1e-06)
        for c in range(2):
            for j in range(length // LANES):
                ls = slice(j * LANES, (j + 1) * LANES)
                rows = [ref[c] if j == 0 else ref[c, :, ls] for ref in (head_refs if j == 0 else image_refs)]
                out_ref[0, c, :, ls] = (jnp.concatenate(rows, axis=0) * scale).astype(BF16)

    return pl.pallas_call(
        kernel,
        in_specs=[VMEM] * (2 * number + count),
        out_shape=jax.ShapeDtypeStruct((1, 2, total_rows, length), BF16),
        compiler_params=pltpu.CompilerParams(vmem_limit_bytes=12 * 2**20),
        name="finish",
    )(*images, *heads, *energies)


def cyclic(value, axis, steps):
    count = lax.axis_size(axis)
    return lax.ppermute(value, axis, [(i, (i + steps) % count) for i in range(count)])


def plan(per):
    if per == 96:
        return [16, 32, 48], [[0, 1], [2]], [24, 48, 24]
    return [per], [[0]], [per]


def strip(echoes, range_filter, rcmc_weights, fm_rate, rcmc_shift, seam_width, seam_link):
    count = lax.axis_size("line")
    chips = lax.axis_size("chip")
    me = lax.axis_index("line").astype(jnp.int32)
    lines = echoes.shape[2]
    length = lines * count
    columns = length // LANES
    per = fm_rate.shape[1]

    turn = root(count, np.outer(np.arange(count), np.arange(columns)), -1)
    base = column_twiddle(columns, length, -1).astype(np.float64)
    tw_all = np.stack([
        turn[0][:, :, None] * base[0] - turn[1][:, :, None] * base[1],
        turn[0][:, :, None] * base[1] + turn[1][:, :, None] * base[0]], axis=1).astype(np.float32)
    tw_forward = lax.dynamic_index_in_dim(jnp.asarray(tw_all), me, 0, keepdims=False)
    tw_inverse = column_twiddle(columns, length, 1, 1.0 / length)
    mat_forward = lane_matrix(-1)
    mat_inverse = lane_matrix(1)

    me1 = me.reshape(1)
    sizes, groups, splits = plan(per)
    starts = [sum(sizes[:c]) for c in range(len(sizes))]
    chunks = []
    for c, (begin, rows) in enumerate(zip(starts, sizes)):
        if c == 0:
            outs, g, x = compress_first(echoes, range_filter, me1, count, per, rows)
        else:
            outs = compress(x, g, me1, count, per, begin, rows, chunks[-1][0])
        pieces = [outs[0]]
        for s in range(1, count):
            pieces.append(cyclic(outs[s], "line", s))
        chunks.append(pieces)

    *phase, weights = phases(fm_rate[0], rcmc_weights, columns, splits)
    seam = jnp.concatenate([seam_width, seam_link])

    dop, images, heads, tails, energies = [], [], [], [], []
    begun = 0
    below = None
    blocks = []
    for n, group in enumerate(groups):
        after = [phase[0]] if n == 0 else energies[-1:]
        outs = doppler([chunks[c] for c in group], tw_forward, mat_forward, MARGIN if n == 0 else 0, after)
        dop.append(outs[0])
        blocks.append((starts[group[0]], outs[0].shape[2]))
        if n == 0:
            below = lax.ppermute(outs[1], "line", [(i, i - 1) for i in range(1, count)])
        held = sum(blocks[-1])
        while len(images) < len(splits):
            rows, factor = splits[len(images)], phase[len(images)]
            need = begun + rows + MARGIN
            if need > held and held < per:
                break
            parts = []
            for d, (b, n) in zip(dop, blocks):
                low, high = max(b, begun), min(b + n, -(-need // 8) * 8)
                if low < high:
                    parts.append((d, low - b, high - low))
            if need > per:
                parts.append((below, 0, MARGIN))
            i = len(images)
            image, head, tail, energy = focus_rows(
                parts, weights, rcmc_shift[0], factor, tw_inverse, mat_inverse, begun, rows,
                tails if i == len(splits) - 1 else [])
            images.append(image)
            heads.append(head)
            energies.append(energy)
            tails.append(tail)
            begun += rows
    earlier = lax.ppermute(tails[-1], "chip", [(j, j + 1) for j in range(chips - 1)])
    *mixed, energy = blend(heads, earlier, energies, seam)
    everyone = [energy] + [cyclic(energy, "line", s) for s in range(1, count)]
    return finish(images, mixed, everyone, float(RKEEP * length))


def solution(mesh):
    in_specs = (
        P("chip", None, "line", None),
        P(),
        P(),
        P("chip", "line"),
        P("chip", "line"),
        P("chip"),
        P("chip"),
    )
    out_specs = P("chip", None, "line", None)
    return jax.shard_map(strip, mesh=mesh, in_specs=in_specs, out_specs=out_specs, check_vma=False)
```

time: 532 us -> 146 us (0.27); the launches traced: 522 us -> 144 us
  matrix products: 164 us -> 0 us
  other arithmetic: 145 us -> 0.08 us
  local copies, waits for them, and re-layouts: 129 us -> 8.37 us
  Pallas kernels: 0 us -> 54.1 us
  blocking collectives: 11.4 us -> 0 us
  starting transfers between devices: 12.4 us -> 22.1 us
    dot_general x8 -> x0, matrix products: 164 us -> none  [complex_einsum(): jnp.einsum(form, pair, stacked_table(table), precision=lax.Precision.HIGH...]
    sub x6 -> x0, other arithmetic: 60.4 us -> none  [complex_scale(): pair[0] * factor_real - pair[1] * factor_imag]
    pallas_call x0 -> x11, Pallas kernels: none -> 54.1 us  [the longest x2 28.2 us: compress(): pl.pallas_call(kernel, in_specs=[pl.BlockSpec(memory_space=pltpu.SMEM), V...]
    ppermute x2 -> x14, waiting for transfers between devices: 14 us -> 57.6 us  [the longest x12 52.7 us: cyclic(): lax.ppermute(value, axis, [(i, (i + steps) % count) for i in range(count)])]
    all_to_all x1 -> x0, waiting for transfers between devices: 43.6 us -> none  [local(): lax.all_to_all(compressed, 'line', split_axis=1, concat_axis=2, tiled=True)]
    another operation x9 -> x0, other arithmetic: 37.9 us -> none  [the longest x4 37.9 us: complex_scale(): jnp.stack([pair[0] * factor_real - pair[1] * factor_imag, pair[0] * facto...]
    gather x9 -> x0, local copies, waits for them, and re-layouts: 37.2 us -> none  [the longest x8 35.4 us: local(): picked = jnp.take(extended, positions + offset, axis=1)]
    another operation x3 -> x0, local copies, waits for them, and re-layouts: 34.1 us -> none  [the longest x1 33.9 us: complex_scale(): jnp.stack([pair[0] * factor_real - pair[1] * factor_imag, pair[0] * facto...]
  transfers between devices with their start and end apart: 3 -> 14, of which waited for: 3 -> 6; matrix products, arithmetic and copies ran while one was open for 5% -> 1% of each run, Pallas kernels for 0% -> 27%
where the time goes in v1:
time: 146 us; the launch traced here: 144 us
  waiting for transfers between devices  57.6 us (39%)
  Pallas kernels  54.1 us (37%)
  starting transfers between devices  22.1 us (15%)
  local copies, waits for them, and re-layouts  8.37 us (6%)
  between operations  1.49 us (1%)
    ppermute x12, waiting for transfers between devices, cyclic(): lax.ppermute(value, axis, [(i, (i + steps) % count) for i in range(count)])  52.7 us
    pallas_call x2, Pallas kernels, compress(): pl.pallas_call(kernel, in_specs=[pl.BlockSpec(memory_space=pltpu.SMEM), V...  28.2 us
    ppermute x12, starting transfers between devices, cyclic(): lax.ppermute(value, axis, [(i, (i + steps) % count) for i in range(count)])  17.9 us
    pallas_call x3, Pallas kernels, focus_rows(): pl.pallas_call(kernel, in_specs=[pl.BlockSpec(memory_space=pltpu.SMEM)] +...  9.11 us
    pallas_call x1, Pallas kernels, compress_first(): pl.pallas_call(kernel, in_specs=[pl.BlockSpec(memory_space=pltpu.SMEM), h...  8.66 us
    unnamed x22, local copies, waits for them, and re-layouts  7.53 us
    ppermute x1, waiting for transfers between devices, strip(): lax.ppermute(tails[-1], 'chip', [(j, j + 1) for j in range(chips - 1)])  4.83 us
    pallas_call x1, Pallas kernels, phases(): pl.pallas_call(kernel, grid=(columns // together,), in_specs=[pl.BlockSpe...  3.43 us
  transfers between devices with their start and end apart: 14, of which 6 were waited for; matrix products, arithmetic and copies ran while one was open for 1% of the time, Pallas kernels for 27%

profile of v1, /device:TPU:12, one launch (start us, length us, event | category | flops | bytes accessed | tf_op | source)
XLA Modules:
  0.0 143.7 jit_solution(15516927933791916170)
XLA Ops:
  0.0 0.8 copy-done.6
  0.8 1.0 copy-done.7
  1.7 8.7 %compress.3 = (f32[2,16,1024]{2,1,0:T(8,128)S(1)}, f32[2,16,1024]{2,1,0:T(8,128)S(1)}, f32[2,16,1024]{2,1,0:T(8,128)S(1)}, f32[2,16,1024]{2,1,0:T(8,128)S(1)}, f...) custom-call(s32[1]{0:T(128)} %bitcast.1.me_ref, bf16[1,2,1024,4096]{3,2,1,0:T(8,128)(2,1)} %x_hbm.1, ...), custom_call_target="tpu_custom_call" | custom-call | flops 8589934592 | bytes 16777216 | tf_op jit(solution)/shard_map/compress/pallas_call | solution.py:246
  10.4 1.6 %collective-permute-start = (f32[2,16,1024]{2,1,0:T(8,128)S(1)}, f32[2,16,1024]{2,1,0:T(8,128)S(1)}, u32[]{:S(2)}, u32[]{:S(2)}) collective-permute-start(f32[2,16,1024]{2,1,0:T(8,128)S(1)} %get-tuple-element.42), channel_id=1, source_target_pairs={{0,1},{1,2},{2,3},{3,0},{4,5},{5,6},{6,7},{7,4},{8,9},{9,10},{10,1... | collective-permute-start | bytes 393224 | tf_op jit(solution)/shard_map/ppermute | solution.py:614
  12.0 11.6 %compress.4 = (f32[2,32,1024]{2,1,0:T(8,128)S(1)}, f32[2,32,1024]{2,1,0:T(8,128)S(1)}, f32[2,32,1024]{2,1,0:T(8,128)S(1)}, f32[2,32,1024]{2,1,0:T(8,128)S(1)}) custom-call(s32[1]{0:T(128)} %bitcast.1.me_ref, bf16[2,1024,4096]{2,1,0:T(8,128)(2,1)S(1)} %get-tuple-element.45.x_ref, f32[2,32,128]{2,1,0:T(8,128)S(1)} %get-tuple-element.46.g_ref, ...), custom_call_target="tpu_custom_call" | custom-call | flops 17179869184 | bytes 16777216 | tf_op jit(solution)/shard_map/compress/pallas_call | solution.py:289
  23.6 0.0 copy-done.8
  23.6 1.6 %collective-permute-start.3 = (f32[2,32,1024]{2,1,0:T(8,128)S(1)}, f32[2,32,1024]{2,1,0:T(8,128)S(1)}, u32[]{:S(2)}, u32[]{:S(2)}) collective-permute-start(f32[2,32,1024]{2,1,0:T(8,128)S(1)} %get-tuple-element.48), channel_id=1, source_target_pairs={{0,1},{1,2},{2,3},{3,0},{4,5},{5,6},{6,7},{7,4},{8,9},{9,10},{10,1... | collective-permute-start | bytes 786440 | tf_op jit(solution)/shard_map/ppermute | solution.py:614
  25.2 1.3 collective-permute-start.4
  26.5 0.5 collective-permute-start.5
  26.9 1.7 %collective-permute-start.1 = (f32[2,16,1024]{2,1,0:T(8,128)S(1)}, f32[2,16,1024]{2,1,0:T(8,128)S(1)}, u32[]{:S(2)}, u32[]{:S(2)}) collective-permute-start(f32[2,16,1024]{2,1,0:T(8,128)S(1)} %get-tuple-element.43), channel_id=1, source_target_pairs={{0,2},{1,3},{2,0},{3,1},{4,6},{5,7},{6,4},{7,5},{8,10},{9,11},{10,... | collective-permute-start | bytes 393224 | tf_op jit(solution)/shard_map/ppermute | solution.py:614
  28.6 0.0 collective-permute-done.refs_1_
  28.6 1.4 collective-permute-start.2
  30.0 0.1 broadcast_in_dim.8.fm_ref
  30.1 3.4 %phases.1 = (f32[2,32,24,128]{3,2,1,0:T(8,128)S(1)}, f32[2,32,48,128]{3,2,1,0:T(8,128)S(1)}, f32[2,32,24,128]{3,2,1,0:T(8,128)S(1)}, f32[256,128]{1,0:T(8,128)S(1)}) custom-call(f32[96,128]{1,0:T(8,128)S(1)} %broadcast_in_dim.8.fm_ref, f32[8,4096]{1,0:T(8,128)S(1)} %copy-done.3, f32[128,128]{1,0:T(8,128)S(1)} %copy-done.4), custom_call_target="tpu_custom_call" | custom-call | flops 23592960 | bytes 3145728 | tf_op jit(solution)/shard_map/phases/pallas_call | solution.py:425
  33.5 0.8 dynamic-slice_bitcast_fusion.refs_8_.refs_4_
  34.3 21.5 %collective-permute-done.1.refs_2_ = f32[2,16,1024]{2,1,0:T(8,128)S(1)} collective-permute-done((f32[2,16,1024]{2,1,0:T(8,128)S(1)}, f32[2,16,1024]{2,1,0:T(8,128)S(1)}, u32[]{:S(2)}, u32[]{:S(2)}) %collective-permute-start.1) | collective-permute-done | bytes 131104 | tf_op jit(solution)/shard_map/ppermute | solution.py:614
  55.8 1.8 %collective-permute-done.2.refs_3_ = f32[2,16,1024]{2,1,0:T(8,128)S(1)} collective-permute-done((f32[2,16,1024]{2,1,0:T(8,128)S(1)}, f32[2,16,1024]{2,1,0:T(8,128)S(1)}, u32[]{:S(2)}, u32[]{:S(2)}) %collective-permute-start.2) | collective-permute-done | bytes 131104 | tf_op jit(solution)/shard_map/ppermute | solution.py:614
  57.6 0.0 collective-permute-done.3.refs_5_
  57.6 0.0 collective-permute-done.4.refs_6_
  57.6 0.0 collective-permute-done.5.refs_7_
  57.6 1.2 doppler.2
  58.9 0.0 copy-start
  58.9 0.0 copy-start.2
  58.9 0.0 copy-start.5
  58.9 2.2 %collective-permute-start.9 = (f32[1216,128]{1,0:T(8,128)S(1)}, f32[1216,128]{1,0:T(8,128)S(1)}, u32[]{:S(2)}, u32[]{:S(2)}) collective-permute-start(f32[1216,128]{1,0:T(8,128)S(1)} %get-tuple-element.62), channel_id=1, source_target_pairs={{1,0},{2,1},{3,2},{5,4},{6,5},{7,6},{9,8},{10,9},{11,10},{13,12},{... | collective-permute-start | bytes 1867784 | tf_op jit(solution)/shard_map/ppermute | solution.py:669
  61.1 5.8 %copy-done.9 = bf16[2,1024,4096]{2,1,0:T(8,128)(2,1)S(1)} copy-done((bf16[2,1024,4096]{2,1,0:T(8,128)(2,1)S(1)}, bf16[2,1024,4096]{2,1,0:T(8,128)(2,1)}, u32[]{:S(2)}) %copy-start.9) | copy-done | bytes 16777240
  66.9 16.7 %compress.5 = (f32[2,48,1024]{2,1,0:T(8,128)S(1)}, f32[2,48,1024]{2,1,0:T(8,128)S(1)}, f32[2,48,1024]{2,1,0:T(8,128)S(1)}, f32[2,48,1024]{2,1,0:T(8,128)S(1)}) custom-call(s32[1]{0:T(128)} %bitcast.1.me_ref, bf16[2,1024,4096]{2,1,0:T(8,128)(2,1)S(1)} %copy-done.9, f32[2,32,128]{2,1,0:T(8,128)S(1)} %get-tuple-element.46.g_ref, ...), custom_call_target="tpu_custom_call" | custom-call | flops 25769803776 | bytes 16777216 | tf_op jit(solution)/shard_map/compress/pallas_call | solution.py:289
  83.6 2.1 %collective-permute-start.6 = (f32[2,48,1024]{2,1,0:T(8,128)S(1)}, f32[2,48,1024]{2,1,0:T(8,128)S(1)}, u32[]{:S(2)}, u32[]{:S(2)}) collective-permute-start(f32[2,48,1024]{2,1,0:T(8,128)S(1)} %get-tuple-element.56), channel_id=1, source_target_pairs={{0,1},{1,2},{2,3},{3,0},{4,5},{5,6},{6,7},{7,4},{8,9},{9,10},{10,1... | collective-permute-start | bytes 1179656 | tf_op jit(solution)/shard_map/ppermute | solution.py:614
  85.6 0.0 collective-permute-start.7
  85.6 1.5 %collective-permute-start.8 = (f32[2,48,1024]{2,1,0:T(8,128)S(1)}, f32[2,48,1024]{2,1,0:T(8,128)S(1)}, u32[]{:S(2)}, u32[]{:S(2)}) collective-permute-start(f32[2,48,1024]{2,1,0:T(8,128)S(1)} %get-tuple-element.58), channel_id=1, source_target_pairs={{0,3},{1,0},{2,1},{3,2},{4,7},{5,4},{6,5},{7,6},{8,11},{9,8},{10,9... | collective-permute-start | bytes 1179656 | tf_op jit(solution)/shard_map/ppermute | solution.py:614
  88.5 2.6 %focus.3 = (f32[2,24,4096]{2,1,0:T(8,128)S(1)}, f32[2,24,128]{2,1,0:T(8,128)S(1)}, f32[2,24,128]{2,1,0:T(8,128)S(1)}, f32[8,128]{1,0:T(8,128)S(1)}) custom-call(s32[96]{0:T(128)S(1)} %bitcast.5, f32[2,32,48,128]{3,2,1,0:T(8,128)S(1)} %get-tuple-element.52.refs_0_, f32[256,128]{1,0:T(8,128)S(1)} %get-tuple-element.53.refs_1_.refs_2_, ...), custom_call_target="tpu_custom_call" | custom-call | flops 301989888 | bytes 3145728 | tf_op jit(solution)/shard_map/focus/pallas_call | solution.py:526
  91.1 20.9 %collective-permute-done.6.refs_1_ = f32[2,48,1024]{2,1,0:T(8,128)S(1)} collective-permute-done((f32[2,48,1024]{2,1,0:T(8,128)S(1)}, f32[2,48,1024]{2,1,0:T(8,128)S(1)}, u32[]{:S(2)}, u32[]{:S(2)}) %collective-permute-start.6) | collective-permute-done | bytes 393248 | tf_op jit(solution)/shard_map/ppermute | solution.py:614
  112.0 7.2 %collective-permute-done.7.refs_2_ = f32[2,48,1024]{2,1,0:T(8,128)S(1)} collective-permute-done((f32[2,48,1024]{2,1,0:T(8,128)S(1)}, f32[2,48,1024]{2,1,0:T(8,128)S(1)}, u32[]{:S(2)}, u32[]{:S(2)}) %collective-permute-start.7) | collective-permute-done | bytes 393248 | tf_op jit(solution)/shard_map/ppermute | solution.py:614
  119.2 0.0 collective-permute-done.8.refs_3_
  119.2 1.2 doppler.3.refs_1_.refs_0_
  120.4 3.9 %focus.4 = (f32[2,48,4096]{2,1,0:T(8,128)S(1)}, f32[2,48,128]{2,1,0:T(8,128)S(1)}, f32[2,48,128]{2,1,0:T(8,128)S(1)}, f32[8,128]{1,0:T(8,128)S(1)}) custom-call(s32[96]{0:T(128)S(1)} %bitcast.6, f32[2,32,48,128]{3,2,1,0:T(8,128)S(1)} %get-tuple-element.52.refs_0_, f32[2,32,48,128]{3,2,1,0:T(8,128)S(1)} %doppler.3.refs_1_.refs_0_, ...), custom_call_target="tpu_custom_call" | custom-call | flops 603979776 | bytes 6291456 | tf_op jit(solution)/shard_map/focus/pallas_call | solution.py:526
  124.3 0.0 collective-permute-done.9.refs_1_
  124.3 2.6 %focus.5 = (f32[2,24,4096]{2,1,0:T(8,128)S(1)}, f32[2,24,128]{2,1,0:T(8,128)S(1)}, f32[2,96,128]{2,1,0:T(8,128)S(1)}, f32[8,128]{1,0:T(8,128)S(1)}) custom-call(s32[96]{0:T(128)S(1)} %bitcast.7, f32[2,32,48,128]{3,2,1,0:T(8,128)S(1)} %doppler.3.refs_1_.refs_0_, f32[1216,128]{1,0:T(8,128)S(1)} %collective-permute-done.9.refs_1_, ...), custom_call_target="tpu_custom_call" | custom-call | flops 301989888 | bytes 3145728 | tf_op jit(solution)/shard_map/focus/pallas_call | solution.py:526
  127.0 1.9 %collective-permute-start.10 = (f32[2,96,128]{2,1,0:T(8,128)S(1)}, f32[2,96,128]{2,1,0:T(8,128)S(1)}, u32[]{:S(2)}, u32[]{:S(2)}) collective-permute-start(f32[2,96,128]{2,1,0:T(8,128)S(1)} %get-tuple-element.70), channel_id=1, source_target_pairs={{0,4},{4,8},{8,12},{12,16},{16,20},{20,24},{24,28},{1,5},{5,9},{9,... | collective-permute-start | bytes 294920 | tf_op jit(solution)/shard_map/ppermute | solution.py:692
  128.9 0.1 pad_add_fusion.seam_ref
  129.0 4.8 %collective-permute-done.10.refs_3_ = f32[2,96,128]{2,1,0:T(8,128)S(1)} collective-permute-done((f32[2,96,128]{2,1,0:T(8,128)S(1)}, f32[2,96,128]{2,1,0:T(8,128)S(1)}, u32[]{:S(2)}, u32[]{:S(2)}) %collective-permute-start.10) | collective-permute-done | bytes 98336 | tf_op jit(solution)/shard_map/ppermute | solution.py:692
  133.8 0.6 blend.1
  134.4 0.1 collective-permute-start.13
  134.5 3.4 %collective-permute-start.12 = (f32[8,128]{1,0:T(8,128)S(1)}, f32[8,128]{1,0:T(8,128)S(1)}, u32[]{:S(2)}, u32[]{:S(2)}) collective-permute-start(f32[8,128]{1,0:T(8,128)S(1)} %get-tuple-element.76.refs_6_), channel_id=1, source_target_pairs={{0,2},{1,3},{2,0},{3,1},{4,6},{5,7},{6,4},{7,5},{8,10},{9,11},{10,... | collective-permute-start | bytes 12296 | tf_op jit(solution)/shard_map/ppermute | solution.py:614
  137.9 2.8 %collective-permute-start.11 = (f32[8,128]{1,0:T(8,128)S(1)}, f32[8,128]{1,0:T(8,128)S(1)}, u32[]{:S(2)}, u32[]{:S(2)}) collective-permute-start(f32[8,128]{1,0:T(8,128)S(1)} %get-tuple-element.76.refs_6_), channel_id=1, source_target_pairs={{0,1},{1,2},{2,3},{3,0},{4,5},{5,6},{6,7},{7,4},{8,9},{9,10},{10,1... | collective-permute-start | bytes 12296 | tf_op jit(solution)/shard_map/ppermute | solution.py:614
  140.8 0.0 collective-permute-done.13.refs_9_
  140.8 1.3 collective-permute-done.11.refs_7_
  142.1 1.6 %finish.1 = bf16[1,2,96,4096]{3,2,1,0:T(8,128)(2,1)} custom-call(f32[2,24,4096]{2,1,0:T(8,128)S(1)} %get-tuple-element.54.refs_0_, f32[2,48,4096]{2,1,0:T(8,128)S(1)} %get-tuple-element.61.refs_1_, f32[2,24,4096]{2,1,0:T(8,128)S(1)} %get-tuple-element.66.refs_2_, f32[2,24,128]{2,1,0:T(8,128)S(1)} %get-tuple-element.73.refs_3_, ...), custom_call_target="tpu_custom_call" | custom-call | tf_op jit(solution)/shard_map/finish/pallas_call | solution.py:603
  (16 shorter events, 0.0 us)
Async XLA Ops:
  0.0 0.8 copy-start.6
  0.8 1.0 copy-start.7
  10.4 13.2 %copy-start.8 = (bf16[2,1024,4096]{2,1,0:T(8,128)(2,1)}, bf16[2,1024,4096]{2,1,0:T(8,128)(2,1)S(1)}, u32[]{:S(2)}) copy-start(bf16[2,1024,4096]{2,1,0:T(8,128)(2,1)S(1)} %get-tuple-element.45.x_ref) | copy-start | bytes 50331652
  10.4 18.2 %collective-permute-start = (f32[2,16,1024]{2,1,0:T(8,128)S(1)}, f32[2,16,1024]{2,1,0:T(8,128)S(1)}, u32[]{:S(2)}, u32[]{:S(2)}) collective-permute-start(f32[2,16,1024]{2,1,0:T(8,128)S(1)} %get-tuple-element.42), channel_id=1, source_target_pairs={{0,1},{1,2},{2,3},{3,0},{4,5},{5,6},{6,7},{7,4},{8,9},{9,10},{10,1... | collective-permute-start | bytes 393224 | tf_op jit(solution)/shard_map/ppermute | solution.py:614
  12.0 18.0 %copy-start.10 = (f32[1,96]{1,0:T(1,128)S(1)}, f32[1,96]{1,0:T(1,128)}, u32[]{:S(2)}) copy-start(f32[1,96]{1,0:T(1,128)} %param.16) | copy-start | bytes 1156
  12.0 18.0 %copy-start.3 = (f32[8,4096]{1,0:T(8,128)S(1)}, f32[8,4096]{1,0:T(8,128)}, u32[]{:S(2)}) copy-start(f32[8,4096]{1,0:T(8,128)} %w_ref.1) | copy-start | bytes 393220
  12.0 18.0 %copy-start.4 = (f32[128,128]{1,0:T(8,128)S(1)}, f32[128,128]{1,0:T(8,128)}, u32[]{:S(2)}) copy-start(f32[128,128]{1,0:T(8,128)} %constant.24.clone.pick_ref) | copy-start | bytes 196612
  12.0 45.6 %copy-start.1 = (bf16[768,256]{1,0:T(8,128)(2,1)S(1)}, bf16[768,256]{1,0:T(8,128)(2,1)}, u32[]{:S(2)}) copy-start(bf16[768,256]{1,0:T(8,128)(2,1)} %constant.25.clone.refs_9_.refs_5_) | copy-start | bytes 1179652
  23.6 34.0 %collective-permute-start.3 = (f32[2,32,1024]{2,1,0:T(8,128)S(1)}, f32[2,32,1024]{2,1,0:T(8,128)S(1)}, u32[]{:S(2)}, u32[]{:S(2)}) collective-permute-start(f32[2,32,1024]{2,1,0:T(8,128)S(1)} %get-tuple-element.48), channel_id=1, source_target_pairs={{0,1},{1,2},{2,3},{3,0},{4,5},{5,6},{6,7},{7,4},{8,9},{9,10},{10,1... | collective-permute-start | bytes 786440 | tf_op jit(solution)/shard_map/ppermute | solution.py:614
  25.2 32.4 %collective-permute-start.4 = (f32[2,32,1024]{2,1,0:T(8,128)S(1)}, f32[2,32,1024]{2,1,0:T(8,128)S(1)}, u32[]{:S(2)}, u32[]{:S(2)}) collective-permute-start(f32[2,32,1024]{2,1,0:T(8,128)S(1)} %get-tuple-element.49), channel_id=1, source_target_pairs={{0,2},{1,3},{2,0},{3,1},{4,6},{5,7},{6,4},{7,5},{8,10},{9,11},{10,... | collective-permute-start | bytes 786440 | tf_op jit(solution)/shard_map/ppermute | solution.py:614
  26.5 31.1 %collective-permute-start.5 = (f32[2,32,1024]{2,1,0:T(8,128)S(1)}, f32[2,32,1024]{2,1,0:T(8,128)S(1)}, u32[]{:S(2)}, u32[]{:S(2)}) collective-permute-start(f32[2,32,1024]{2,1,0:T(8,128)S(1)} %get-tuple-element.50), channel_id=1, source_target_pairs={{0,3},{1,0},{2,1},{3,2},{4,7},{5,4},{6,5},{7,6},{8,11},{9,8},{10,9... | collective-permute-start | bytes 786440 | tf_op jit(solution)/shard_map/ppermute | solution.py:614
  26.9 28.9 %collective-permute-start.1 = (f32[2,16,1024]{2,1,0:T(8,128)S(1)}, f32[2,16,1024]{2,1,0:T(8,128)S(1)}, u32[]{:S(2)}, u32[]{:S(2)}) collective-permute-start(f32[2,16,1024]{2,1,0:T(8,128)S(1)} %get-tuple-element.43), channel_id=1, source_target_pairs={{0,2},{1,3},{2,0},{3,1},{4,6},{5,7},{6,4},{7,5},{8,10},{9,11},{10,... | collective-permute-start | bytes 393224 | tf_op jit(solution)/shard_map/ppermute | solution.py:614
  28.6 29.0 %collective-permute-start.2 = (f32[2,16,1024]{2,1,0:T(8,128)S(1)}, f32[2,16,1024]{2,1,0:T(8,128)S(1)}, u32[]{:S(2)}, u32[]{:S(2)}) collective-permute-start(f32[2,16,1024]{2,1,0:T(8,128)S(1)} %get-tuple-element.44), channel_id=1, source_target_pairs={{0,3},{1,0},{2,1},{3,2},{4,7},{5,4},{6,5},{7,6},{8,11},{9,8},{10,9... | collective-permute-start | bytes 393224 | tf_op jit(solution)/shard_map/ppermute | solution.py:614
  58.9 29.6 %copy-start = (bf16[768,256]{1,0:T(8,128)(2,1)S(1)}, bf16[768,256]{1,0:T(8,128)(2,1)}, u32[]{:S(2)}) copy-start(bf16[768,256]{1,0:T(8,128)(2,1)} %constant.27.clone.refs_4_.refs_5_) | copy-start | bytes 1179652
  58.9 29.6 %copy-start.2 = (f32[2,32,128]{2,1,0:T(8,128)S(1)}, f32[2,32,128]{2,1,0:T(8,128)}, u32[]{:S(2)}) copy-start(f32[2,32,128]{2,1,0:T(8,128)} %constant.26.clone.refs_3_.refs_4_) | copy-start | bytes 98308
  58.9 29.6 %copy-start.5 = (s32[1,96]{1,0:T(1,128)S(1)}, s32[1,96]{1,0:T(1,128)}, u32[]{:S(2)}) copy-start(s32[1,96]{1,0:T(1,128)} %param.17) | copy-start | bytes 1156
  58.9 65.4 %collective-permute-start.9 = (f32[1216,128]{1,0:T(8,128)S(1)}, f32[1216,128]{1,0:T(8,128)S(1)}, u32[]{:S(2)}, u32[]{:S(2)}) collective-permute-start(f32[1216,128]{1,0:T(8,128)S(1)} %get-tuple-element.62), channel_id=1, source_target_pairs={{1,0},{2,1},{3,2},{5,4},{6,5},{7,6},{9,8},{10,9},{11,10},{13,12},{... | collective-permute-start | bytes 1867784 | tf_op jit(solution)/shard_map/ppermute | solution.py:669
  61.1 5.8 %copy-start.9 = (bf16[2,1024,4096]{2,1,0:T(8,128)(2,1)S(1)}, bf16[2,1024,4096]{2,1,0:T(8,128)(2,1)}, u32[]{:S(2)}) copy-start(bf16[2,1024,4096]{2,1,0:T(8,128)(2,1)} %copy-done.8) | copy-start | bytes 50331652
  83.6 28.4 %collective-permute-start.6 = (f32[2,48,1024]{2,1,0:T(8,128)S(1)}, f32[2,48,1024]{2,1,0:T(8,128)S(1)}, u32[]{:S(2)}, u32[]{:S(2)}) collective-permute-start(f32[2,48,1024]{2,1,0:T(8,128)S(1)} %get-tuple-element.56), channel_id=1, source_target_pairs={{0,1},{1,2},{2,3},{3,0},{4,5},{5,6},{6,7},{7,4},{8,9},{9,10},{10,1... | collective-permute-start | bytes 1179656 | tf_op jit(solution)/shard_map/ppermute | solution.py:614
  85.6 33.6 %collective-permute-start.7 = (f32[2,48,1024]{2,1,0:T(8,128)S(1)}, f32[2,48,1024]{2,1,0:T(8,128)S(1)}, u32[]{:S(2)}, u32[]{:S(2)}) collective-permute-start(f32[2,48,1024]{2,1,0:T(8,128)S(1)} %get-tuple-element.57), channel_id=1, source_target_pairs={{0,2},{1,3},{2,0},{3,1},{4,6},{5,7},{6,4},{7,5},{8,10},{9,11},{10,... | collective-permute-start | bytes 1179656 | tf_op jit(solution)/shard_map/ppermute | solution.py:614
  85.6 33.6 %collective-permute-start.8 = (f32[2,48,1024]{2,1,0:T(8,128)S(1)}, f32[2,48,1024]{2,1,0:T(8,128)S(1)}, u32[]{:S(2)}, u32[]{:S(2)}) collective-permute-start(f32[2,48,1024]{2,1,0:T(8,128)S(1)} %get-tuple-element.58), channel_id=1, source_target_pairs={{0,3},{1,0},{2,1},{3,2},{4,7},{5,4},{6,5},{7,6},{8,11},{9,8},{10,9... | collective-permute-start | bytes 1179656 | tf_op jit(solution)/shard_map/ppermute | solution.py:614
  127.0 6.8 %collective-permute-start.10 = (f32[2,96,128]{2,1,0:T(8,128)S(1)}, f32[2,96,128]{2,1,0:T(8,128)S(1)}, u32[]{:S(2)}, u32[]{:S(2)}) collective-permute-start(f32[2,96,128]{2,1,0:T(8,128)S(1)} %get-tuple-element.70), channel_id=1, source_target_pairs={{0,4},{4,8},{8,12},{12,16},{16,20},{20,24},{24,28},{1,5},{5,9},{9,... | collective-permute-start | bytes 294920 | tf_op jit(solution)/shard_map/ppermute | solution.py:692
  134.4 6.4 %collective-permute-start.13 = (f32[8,128]{1,0:T(8,128)S(1)}, f32[8,128]{1,0:T(8,128)S(1)}, u32[]{:S(2)}, u32[]{:S(2)}) collective-permute-start(f32[8,128]{1,0:T(8,128)S(1)} %get-tuple-element.76.refs_6_), channel_id=1, source_target_pairs={{0,3},{1,0},{2,1},{3,2},{4,7},{5,4},{6,5},{7,6},{8,11},{9,8},{10,9... | collective-permute-start | bytes 12296 | tf_op jit(solution)/shard_map/ppermute | solution.py:614
  134.5 6.3 %collective-permute-start.12 = (f32[8,128]{1,0:T(8,128)S(1)}, f32[8,128]{1,0:T(8,128)S(1)}, u32[]{:S(2)}, u32[]{:S(2)}) collective-permute-start(f32[8,128]{1,0:T(8,128)S(1)} %get-tuple-element.76.refs_6_), channel_id=1, source_target_pairs={{0,2},{1,3},{2,0},{3,1},{4,6},{5,7},{6,4},{7,5},{8,10},{9,11},{10,... | collective-permute-start | bytes 12296 | tf_op jit(solution)/shard_map/ppermute | solution.py:614
  137.9 4.2 %collective-permute-start.11 = (f32[8,128]{1,0:T(8,128)S(1)}, f32[8,128]{1,0:T(8,128)S(1)}, u32[]{:S(2)}, u32[]{:S(2)}) collective-permute-start(f32[8,128]{1,0:T(8,128)S(1)} %get-tuple-element.76.refs_6_), channel_id=1, source_target_pairs={{0,1},{1,2},{2,3},{3,0},{4,5},{5,6},{6,7},{7,4},{8,9},{9,10},{10,1... | collective-permute-start | bytes 12296 | tf_op jit(solution)/shard_map/ppermute | solution.py:614

commit v2 on v1

--- a/solution.py
+++ b/solution.py
@@ -14,6 +14,7 @@
 MAXSHIFT = 12
 LANES = 128
 MARGIN = MAXSHIFT + TAPS - 1
+HALO = 24
 
 F32 = jnp.float32
 ANY = pl.BlockSpec(memory_space=pl.ANY)
@@ -32,12 +33,17 @@
     return np.cos(angle), np.sin(angle)
 
 
-def lane_matrix(sign, scale=1.0):
+def lane_matrix():
     index = np.arange(LANES)
-    real, imag = root(LANES, np.outer(index, index), sign)
-    full = scale * np.block([[real, imag], [-imag, real]])
-    high, low = split_np(full)
-    return np.concatenate([high, high, low], axis=0)
+    real, imag = root(LANES, np.outer(index, index), -1)
+    return np.concatenate(split_np(np.block([[real, imag], [-imag, real]])), axis=0)
+
+
+def lane_transform(value, mat_ref):
+    high, low = split3(value)
+    table = mat_ref[...]
+    coarse, fine = table[:2 * LANES], table[2 * LANES:]
+    return dot_nn(jnp.concatenate([high, low, high], axis=1), jnp.concatenate([coarse, coarse, fine], axis=0))
 
 
 def column_twiddle(columns, length, sign, scale=1.0):
@@ -195,7 +201,7 @@
     turned[:, :, :, pl.ds(at, acc.shape[0])] = both.T.reshape(turned.shape[:3] + (acc.shape[0],))
 
 
-def compress_first(echoes, range_filter, me, count, per, rows):
+def compress_first(echoes, range_filter, me, count, per, rows, kept):
     lines, samples = echoes.shape[2], echoes.shape[3]
     columns = samples // LANES
     blocks = max(1, min(4, samples // 1024))
@@ -206,7 +212,7 @@
 
     def kernel(me_ref, x_hbm, f_hbm, t_hbm, *refs):
         outs, refs = refs[:count], refs[count:]
-        g_ref, x_ref, f_ref, t_ref, table, acc, turned, sems = refs
+        g_ref, x_ref, keep_ref, f_ref, t_ref, table, acc, turned, sems = refs
         small = [pltpu.make_async_copy(f_hbm, f_ref, sems.at[2 * blocks]),
                  pltpu.make_async_copy(t_hbm, t_ref, sems.at[2 * blocks + 1])]
         large = []
@@ -240,16 +246,17 @@
 
             lax.fori_loop(0, lines // mblk, body, 0)
         scatter(me_ref, outs, turned)
+        keep_ref[...] = turned[:, kept]
 
     hbm = pl.BlockSpec(memory_space=pltpu.HBM)
     out = jax.ShapeDtypeStruct((2, rows, lines), F32)
     results = pl.pallas_call(
         kernel,
         in_specs=[pl.BlockSpec(memory_space=pltpu.SMEM), hbm, hbm, hbm],
-        out_specs=[VMEM] * (count + 2),
+        out_specs=[VMEM] * (count + 3),
         out_shape=[out] * count + [
             jax.ShapeDtypeStruct((2, columns, LANES), F32),
-            jax.ShapeDtypeStruct((2, lines, samples), BF16)],
+            jax.ShapeDtypeStruct((2, lines, samples), BF16), out],
         scratch_shapes=[
             pltpu.VMEM(range_filter.shape, F32),
             pltpu.VMEM(tables.shape, F32),
@@ -263,18 +270,19 @@
             flops=8 * lines * samples * 2 * width, bytes_accessed=4 * lines * samples, transcendentals=0),
         name="compress",
     )(me, echoes, range_filter, tables)
-    return results[:count], results[count], results[count + 1]
-
-
-def compress(x, g, me, count, per, start, rows, after):
+    return results[:count], *results[count:]
+
+
+def compress(x, g, me, count, per, start, rows, kept, keep=None):
     lines, samples = x.shape[1], x.shape[2]
     columns = samples // LANES
     width = 2 * count * rows
-    mblk = min(256, lines)
-
-    def kernel(me_ref, x_ref, g_ref, _, *refs):
+    mblk = min(512, lines)
+    again = start < MARGIN <= start + rows
+
+    def kernel(me_ref, x_ref, g_ref, keep_ref, *refs):
         outs = refs[:count]
-        table, turned = refs[count:]
+        table, turned = refs[-2:]
         toeplitz(g_ref, table, count, per, start, rows, columns)
 
         def body(m, carry):
@@ -285,61 +293,88 @@
 
         lax.fori_loop(0, lines // mblk, body, 0)
         scatter(me_ref, outs, turned)
+        if again:
+            for c in range(2):
+                refs[count][c * MARGIN:c * MARGIN + start, :] = keep_ref[c]
+                refs[count][c * MARGIN + start:(c + 1) * MARGIN, :] = turned[c, kept, :MARGIN - start, :]
 
     return pl.pallas_call(
         kernel,
-        in_specs=[pl.BlockSpec(memory_space=pltpu.SMEM), VMEM, VMEM, ANY],
-        out_specs=[VMEM] * count,
-        out_shape=[jax.ShapeDtypeStruct((2, rows, lines), F32)] * count,
+        in_specs=[pl.BlockSpec(memory_space=pltpu.SMEM), VMEM, VMEM, VMEM if again else ANY],
+        out_specs=[VMEM] * (count + again),
+        out_shape=[jax.ShapeDtypeStruct((2, rows, lines), F32)] * count
+        + [jax.ShapeDtypeStruct((2 * MARGIN, lines), F32)] * again,
         scratch_shapes=[
             pltpu.VMEM((2, 2 * width, samples), BF16),
             pltpu.VMEM((2, count, rows, lines), F32),
         ],
-        compiler_params=pltpu.CompilerParams(vmem_limit_bytes=(6 + rows * count // 10) * 2**20),
+        compiler_params=pltpu.CompilerParams(vmem_limit_bytes=(9 + rows * count // 10) * 2**20),
         cost_estimate=pl.CostEstimate(
             flops=8 * lines * samples * 2 * width, bytes_accessed=4 * lines * samples, transcendentals=0),
         name="compress",
-    )(me, x, g, after)
-
-
-def doppler(chunks, tw, matrix, lead, after):
+    )(me, x, g, keep)
+
+
+def doppler(chunks, flat, tw, matrix, lead, after):
     count = len(chunks[0])
     lines = chunks[0][0].shape[2]
     sizes = [pieces[0].shape[1] for pieces in chunks]
     rows = sum(sizes)
     own = lines // LANES
     columns = own * count
-    number = count * len(chunks)
+    number = count * len(chunks) + len(flat)
+    total = rows + (HALO if flat else 0)
 
     def kernel(*refs):
         tw_ref, mat_ref = refs[number:number + 2]
         outs, scratch = refs[number + 2 + len(after):-1], refs[-1]
         out_ref = outs[0]
+
+        def group(ins, load, r8, place):
+            inner = [[None] * own for _ in range(count)]
+            for p in range(own):
+                ls = slice(p * LANES, (p + 1) * LANES)
+                spread = dft_list([(load(ref, 0, r8, ls), load(ref, 1, r8, ls)) for ref in ins], 1)
+                for k0 in range(count):
+                    real, imag = root(columns, p * k0, -1)
+                    inner[k0][p] = cmul_const(spread[k0], float(real), float(imag))
+            for k0 in range(count):
+                for k1, (vr, vi) in enumerate(dft_list(inner[k0], -1)):
+                    k = k0 + count * k1
+                    tr = tw_ref[0, k:k + 1, :]
+                    ti = tw_ref[1, k:k + 1, :]
+                    scratch[place(k), :LANES] = vr * tr - vi * ti
+                    scratch[place(k), LANES:] = vr * ti + vi * tr
+
         begun = 0
         for n, size in enumerate(sizes):
             ins = refs[n * count:(n + 1) * count]
-            for r8 in range(0, size, 8):
-                rs = slice(r8, r8 + 8)
-                inner = [[None] * own for _ in range(count)]
-                for p in range(own):
-                    ls = slice(p * LANES, (p + 1) * LANES)
-                    spread = dft_list([(ref[0, rs, ls], ref[1, rs, ls]) for ref in ins], 1)
-                    for k0 in range(count):
-                        real, imag = root(columns, p * k0, -1)
-                        inner[k0][p] = cmul_const(spread[k0], float(real), float(imag))
-                for k0 in range(count):
-                    for k1, (vr, vi) in enumerate(dft_list(inner[k0], -1)):
-                        k = k0 + count * k1
-                        tr = tw_ref[0, k:k + 1, :]
-                        ti = tw_ref[1, k:k + 1, :]
-                        at = k * rows + begun + r8
-                        scratch[at:at + 8, :LANES] = vr * tr - vi * ti
-                        scratch[at:at + 8, LANES:] = vr * ti + vi * tr
+
+            def load(ref, c, r8, ls):
+                return ref[c, pl.ds(r8, 8), ls]
+
+            def body(i, carry, ins=ins, begun=begun):
+                r8 = pl.multiple_of(i * 8, 8)
+                group(ins, load, r8, lambda k: pl.ds(pl.multiple_of(k * total + begun + r8, 8), 8))
+                return carry
+
+            lax.fori_loop(0, size // 8, body, 0)
             begun += size
-        high, low = split3(scratch[...])
-        out = dot_nn(jnp.concatenate([high, low, high], axis=1), mat_ref[...])
-        out_ref[0] = out[:, :LANES].reshape(columns, rows, LANES)
-        out_ref[1] = out[:, LANES:].reshape(columns, rows, LANES)
+        if flat:
+            def load_flat(ref, c, r8, ls):
+                return ref[c * MARGIN + r8:c * MARGIN + r8 + 8, ls]
+
+            for r8 in (*range(0, MARGIN - 8, 8), MARGIN - 8):
+                group(refs[number - count:number], load_flat, r8,
+                      lambda k: slice(k * total + rows + r8, k * total + rows + r8 + 8))
+        out = lane_transform(scratch[...], mat_ref)
+        for c in range(2):
+            part = out[:, c * LANES:(c + 1) * LANES].reshape(columns, total, LANES)
+            out_ref[c] = part[:, :rows, :]
+            if flat:
+                for k in range(columns):
+                    at = (c * columns + k) * MARGIN
+                    outs[-1][at:at + MARGIN, :] = part[k, rows:rows + MARGIN, :]
         if lead:
             for c in range(2):
                 for k in range(columns):
@@ -350,13 +385,13 @@
         kernel,
         in_specs=[VMEM] * (number + 2) + [ANY] * len(after),
         out_shape=[jax.ShapeDtypeStruct((2, columns, rows, LANES), F32)]
-        + ([jax.ShapeDtypeStruct((2 * columns * lead, LANES), F32)] if lead else []),
-        compiler_params=pltpu.CompilerParams(vmem_limit_bytes=16 * 2**20),
-        scratch_shapes=[pltpu.VMEM((columns * rows, 2 * LANES), F32)],
+        + [jax.ShapeDtypeStruct((2 * columns * MARGIN, LANES), F32)] * ((lead > 0) + (len(flat) > 0)),
+        compiler_params=pltpu.CompilerParams(vmem_limit_bytes=(4 + total // 5) * 2**20),
+        scratch_shapes=[pltpu.VMEM((columns * total, 2 * LANES), F32)],
         cost_estimate=pl.CostEstimate(
             flops=2 * columns * rows * 256 * 768, bytes_accessed=16 * columns * rows * LANES, transcendentals=0),
         name="doppler",
-    )(*[piece for pieces in chunks for piece in pieces], tw, matrix, *after)
+    )(*[piece for pieces in chunks for piece in pieces], *flat, tw, matrix, *after)
 
 
 def turn_pair(turns):
@@ -383,7 +418,7 @@
     per = fm.shape[0]
     length = columns * LANES
     coarse = 2048
-    together = 8
+    together = 4
 
     def kernel(fm_ref, w_ref, pick_ref, *outs):
         outs, w_out = outs[:-1], outs[-1]
@@ -437,17 +472,18 @@
     )(jnp.broadcast_to(fm[:, None], (per, LANES)), weights, pick)
 
 
-def focus_rows(parts, weights, shift, phase, tw, matrix, first, rows, earlier):
+def focus_rows(parts, weights, shift, me, mid, phase, tw, matrix, first, rows, earlier):
     columns = phase.shape[1]
-    total = sum(take for _, _, take in parts)
+    total = sum(take for a, _, take in parts if len(a.shape) == 4) + MARGIN
     reach = -(-(rows + MAXSHIFT) // 8) * 8
     pitch_d = max(total, reach + 8)
     pitch_d += 1 - pitch_d % 2
     pitch_u = reach + 1
     pitch_m = rows + 1
 
-    def kernel(shift_ref, *refs):
+    def kernel(shift_ref, me_ref, *refs):
         ins = refs[:len(parts)]
+        middle = me_ref[0] == mid
         w_ref, ph_ref, tw_ref, mat_ref = refs[len(parts):len(parts) + 4]
         before = refs[len(parts) + 4:len(parts) + 4 + len(earlier)]
         out_ref, head_ref, tail_ref, en_ref, dop, sums, moved, scratch = refs[len(parts) + 4 + len(earlier):]
@@ -463,11 +499,14 @@
                 filled = 0
                 for ref, (a, begin, take) in zip(ins, parts):
                     if len(a.shape) == 4:
-                        piece = ref[c, k, begin:begin + take, :]
-                    else:
-                        piece = ref[pl.ds((c * columns + k) * take, take), :]
-                    dop[pl.ds(at + filled, take), :] = piece
-                    filled += take
+                        dop[pl.ds(at + filled, take), :] = ref[c, k, begin:begin + take, :]
+                        filled += take
+                flat = [ref[pl.ds((c * columns + k) * MARGIN, MARGIN), :]
+                        for ref, (a, _, _) in zip(ins, parts) if len(a.shape) == 2]
+                if flat:
+                    piece = jnp.where(middle, flat[1], flat[0]) if len(flat) > 1 else flat[0]
+                    dop[pl.ds(at + filled, MARGIN), :] = piece
+                    filled += MARGIN
                 if filled < reach + 8:
                     dop[pl.ds(at + filled, reach + 8 - filled), :] = jnp.zeros((reach + 8 - filled, LANES), F32)
                 to = (c * columns + k) * pitch_u
@@ -496,36 +535,37 @@
             vr = moved[k * pitch_m:k * pitch_m + rows, :]
             vi = moved[(columns + k) * pitch_m:(columns + k) * pitch_m + rows, :]
             pr, pi = ph_ref[0, k], ph_ref[1, k]
-            scratch[at, :LANES] = vr * pr - vi * pi
-            scratch[at, LANES:] = vr * pi + vi * pr
-        high, low = split3(scratch[...])
-        scratch[...] = dot_nn(jnp.concatenate([high, low, high], axis=1), mat_ref[...])
-        total_energy = jnp.zeros((8, LANES), F32)
-        for r8 in range(0, rows, 8):
+            scratch[at, :LANES] = vr * pi + vi * pr
+            scratch[at, LANES:] = vr * pr - vi * pi
+        scratch[...] = lane_transform(scratch[...], mat_ref)
+
+        def transform(i, total_energy):
+            r8 = pl.multiple_of(i * 8, 8)
+            rs = pl.ds(r8, 8)
             values = []
             for k in range(columns):
-                at = slice(k * rows + r8, k * rows + r8 + 8)
-                vr, vi = scratch[at, :LANES], scratch[at, LANES:]
+                at = pl.ds(pl.multiple_of(k * rows + r8, 8), 8)
+                vi, vr = scratch[at, :LANES], scratch[at, LANES:]
                 tr, ti = tw_ref[0, k:k + 1, :], tw_ref[1, k:k + 1, :]
                 values.append((vr * tr - vi * ti, vr * ti + vi * tr))
-            for j, (vr, vi) in enumerate(dft_list(values, 1)):
+            for j, pair in enumerate(dft_list(values, 1)):
                 ls = slice(j * LANES, (j + 1) * LANES)
-                if j == 0:
-                    head_ref[0, r8:r8 + 8, :] = vr
-                    head_ref[1, r8:r8 + 8, :] = vi
-                else:
-                    out_ref[0, r8:r8 + 8, ls] = vr
-                    out_ref[1, r8:r8 + 8, ls] = vi
-                if j == columns - 1:
-                    tail_ref[0, base + r8:base + r8 + 8, :] = vr
-                    tail_ref[1, base + r8:base + r8 + 8, :] = vi
-                if j > 0:
-                    total_energy = total_energy + vr * vr + vi * vi
+                for c in range(2):
+                    if j == 0:
+                        head_ref[c, rs, :] = pair[c]
+                    else:
+                        out_ref[c, rs, ls] = pair[c]
+                        total_energy = total_energy + pair[c] * pair[c]
+                    if j == columns - 1:
+                        tail_ref[c, pl.ds(pl.multiple_of(base + r8, 8), 8), :] = pair[c]
+            return total_energy
+
+        total_energy = lax.fori_loop(0, rows // 8, transform, jnp.zeros((8, LANES), F32))
         en_ref[...] = total_energy
 
     return pl.pallas_call(
         kernel,
-        in_specs=[pl.BlockSpec(memory_space=pltpu.SMEM)] + [VMEM] * (len(parts) + 4 + len(earlier)),
+        in_specs=[pl.BlockSpec(memory_space=pltpu.SMEM)] * 2 + [VMEM] * (len(parts) + 4 + len(earlier)),
         out_shape=[
             jax.ShapeDtypeStruct((2, rows, columns * LANES), F32),
             jax.ShapeDtypeStruct((2, rows, LANES), F32),
@@ -538,11 +578,11 @@
             pltpu.VMEM((-(-2 * columns * pitch_m // 8) * 8 + 8, LANES), F32),
             pltpu.VMEM((columns * rows, 2 * LANES), F32),
         ],
-        compiler_params=pltpu.CompilerParams(vmem_limit_bytes=(16 if rows < 32 else 30) * 2**20),
+        compiler_params=pltpu.CompilerParams(vmem_limit_bytes=(16 if rows < 32 else 26 if rows < 48 else 32) * 2**20),
         cost_estimate=pl.CostEstimate(
             flops=2 * columns * rows * 256 * 768, bytes_accessed=32 * columns * rows * LANES, transcendentals=0),
         name="focus",
-    )(shift, *[a for a, _, _ in parts], weights, phase, tw, matrix, *earlier)
+    )(shift, me, *[a for a, _, _ in parts], weights, phase, tw, matrix, *earlier)
 
 
 def blend(heads, earlier, energies, seam):
@@ -616,7 +656,7 @@
 
 def plan(per):
     if per == 96:
-        return [16, 32, 48], [[0, 1], [2]], [24, 48, 24]
+        return [16, 16, 32, 32], [[0, 1], [2], [3]], [40, 56]
     return [per], [[0]], [per]
 
 
@@ -636,40 +676,59 @@
         turn[0][:, :, None] * base[1] + turn[1][:, :, None] * base[0]], axis=1).astype(np.float32)
     tw_forward = lax.dynamic_index_in_dim(jnp.asarray(tw_all), me, 0, keepdims=False)
     tw_inverse = column_twiddle(columns, length, 1, 1.0 / length)
-    mat_forward = lane_matrix(-1)
-    mat_inverse = lane_matrix(1)
+    matrix = lane_matrix()
 
     me1 = me.reshape(1)
     sizes, groups, splits = plan(per)
     starts = [sum(sizes[:c]) for c in range(len(sizes))]
-    chunks = []
+    mid = count // 2 - 1
+    raw, chunks = [], []
+    dop, blocks, below = [], [], []
+
+    def azimuth(flat, after):
+        n = len(dop)
+        lead = MARGIN if n == 0 else 0
+        outs = doppler([chunks[c] for c in groups[n]], flat, tw_forward, matrix, lead, after)
+        dop.append(outs[0])
+        blocks.append((starts[groups[n][0]], outs[0].shape[2]))
+        if lead:
+            alone = len(groups) == 1
+            below.append(lax.ppermute(
+                outs[1], "line", [(i, i - 1) for i in range(1, count) if alone or i != mid + 1]))
+        below.extend(outs[1 + (lead > 0):])
+        return outs[-1]
+
     for c, (begin, rows) in enumerate(zip(starts, sizes)):
+        if c == 1:
+            last = keep
+        elif c > 0:
+            last = chunks[-1][0]
         if c == 0:
-            outs, g, x = compress_first(echoes, range_filter, me1, count, per, rows)
+            outs, g, x, keep = compress_first(echoes, range_filter, me1, count, per, rows, mid + 1)
         else:
-            outs = compress(x, g, me1, count, per, begin, rows, chunks[-1][0])
+            outs = compress(x, g, me1, count, per, begin, rows, mid + 1, last)
         pieces = [outs[0]]
         for s in range(1, count):
             pieces.append(cyclic(outs[s], "line", s))
         chunks.append(pieces)
-
+        if len(outs) > count:
+            raw = [outs[count]]
+            for s in range(1, count):
+                raw.append(lax.ppermute(outs[count], "line", [((mid - s) % count, mid)]))
+
+    azimuth([], [])
     *phase, weights = phases(fm_rate[0], rcmc_weights, columns, splits)
     seam = jnp.concatenate([seam_width, seam_link])
 
-    dop, images, heads, tails, energies = [], [], [], [], []
+    images, heads, tails, energies = [], [], [], []
     begun = 0
-    below = None
-    blocks = []
-    for n, group in enumerate(groups):
-        after = [phase[0]] if n == 0 else energies[-1:]
-        outs = doppler([chunks[c] for c in group], tw_forward, mat_forward, MARGIN if n == 0 else 0, after)
-        dop.append(outs[0])
-        blocks.append((starts[group[0]], outs[0].shape[2]))
-        if n == 0:
-            below = lax.ppermute(outs[1], "line", [(i, i - 1) for i in range(1, count)])
+    while len(images) < len(splits):
+        if len(dop) < len(groups):
+            azimuth(raw if len(dop) == 1 else [], [phase[0]] if len(dop) < 2 else energies[-1:])
         held = sum(blocks[-1])
         while len(images) < len(splits):
-            rows, factor = splits[len(images)], phase[len(images)]
+            i = len(images)
+            rows, factor = splits[i], phase[i]
             need = begun + rows + MARGIN
             if need > held and held < per:
                 break
@@ -679,10 +738,9 @@
                 if low < high:
                     parts.append((d, low - b, high - low))
             if need > per:
-                parts.append((below, 0, MARGIN))
-            i = len(images)
+                parts += [(a, 0, MARGIN) for a in below]
             image, head, tail, energy = focus_rows(
-                parts, weights, rcmc_shift[0], factor, tw_inverse, mat_inverse, begun, rows,
+                parts, weights, rcmc_shift[0], me1, mid, factor, tw_inverse, matrix, begun, rows,
                 tails if i == len(splits) - 1 else [])
             images.append(image)
             heads.append(head)

time: 146 us -> 128 us (0.88); the launches traced: 144 us -> 127 us
  waiting for transfers between devices: 57.6 us -> 29.6 us
  starting transfers between devices: 22.1 us -> 33.5 us
    ppermute x12 -> x15, waiting for transfers between devices: 52.7 us -> 24.7 us  [cyclic(): lax.ppermute(value, axis, [(i, (i + steps) % count) for i in range(count)])]
    ppermute x12 -> x15, starting transfers between devices: 17.9 us -> 24.3 us  [cyclic(): lax.ppermute(value, axis, [(i, (i + steps) % count) for i in range(count)])]
    ppermute x1 -> x4, starting transfers between devices: 2.23 us -> 7.25 us  [the longest x3 3.85 us: strip(): raw.append(lax.ppermute(outs[count], 'line', [((mid - s) % count, mid)]))]
    pallas_call x2 -> x3, Pallas kernels: 2.45 us -> 3.98 us  [doppler(): pl.pallas_call(kernel, in_specs=[VMEM] * (number + 2) + [ANY] * len(after...]
    pallas_call x2 -> x3, Pallas kernels: 28.2 us -> 27.3 us  [compress(): pl.pallas_call(kernel, in_specs=[pl.BlockSpec(memory_space=pltpu.SMEM), V...]
    pallas_call x3 -> x2, Pallas kernels: 9.11 us -> 8.41 us  [focus_rows(): pl.pallas_call(kernel, in_specs=[pl.BlockSpec(memory_space=pltpu.SMEM)] *...]
    unnamed x22 -> x20, local copies, waits for them, and re-layouts: 7.53 us -> 7.52 us
  transfers between devices with their start and end apart: 14 -> 20, of which waited for: 6 -> 9; matrix products, arithmetic and copies ran while one was open for 1% -> 1% of each run, Pallas kernels for 27% -> 26%
where the time goes in v2:
time: 128 us; the launch traced here: 127 us
  Pallas kernels  54.1 us (42%)
  starting transfers between devices  33.5 us (26%)
  waiting for transfers between devices  29.6 us (23%)
  local copies, waits for them, and re-layouts  8.36 us (7%)
  between operations  1.56 us (1%)
    pallas_call x3, Pallas kernels, compress(): pl.pallas_call(kernel, in_specs=[pl.BlockSpec(memory_space=pltpu.SMEM), V...  27.3 us
    ppermute x15, waiting for transfers between devices, cyclic(): lax.ppermute(value, axis, [(i, (i + steps) % count) for i in range(count)])  24.7 us
    ppermute x15, starting transfers between devices, cyclic(): lax.ppermute(value, axis, [(i, (i + steps) % count) for i in range(count)])  24.3 us
    pallas_call x1, Pallas kernels, compress_first(): pl.pallas_call(kernel, in_specs=[pl.BlockSpec(memory_space=pltpu.SMEM), h...  8.67 us
    pallas_call x2, Pallas kernels, focus_rows(): pl.pallas_call(kernel, in_specs=[pl.BlockSpec(memory_space=pltpu.SMEM)] *...  8.41 us
    unnamed x20, local copies, waits for them, and re-layouts  7.52 us
    ppermute x1, waiting for transfers between devices, strip(): lax.ppermute(tails[-1], 'chip', [(j, j + 1) for j in range(chips - 1)])  4.83 us
    pallas_call x3, Pallas kernels, doppler(): pl.pallas_call(kernel, in_specs=[VMEM] * (number + 2) + [ANY] * len(after...  3.98 us
  transfers between devices with their start and end apart: 20, of which 9 were waited for; matrix products, arithmetic and copies ran while one was open for 1% of the time, Pallas kernels for 26%

profile of v2, /device:TPU:12, one launch (start us, length us, event | category | flops | bytes accessed | tf_op | source)
XLA Modules:
  0.0 127.2 jit_solution(16861814979011924122)
XLA Ops:
  0.0 0.8 copy-done.5
  0.8 1.0 copy-done.6
  1.7 8.7 %compress.4 = (f32[2,16,1024]{2,1,0:T(8,128)S(1)}, f32[2,16,1024]{2,1,0:T(8,128)S(1)}, f32[2,16,1024]{2,1,0:T(8,128)S(1)}, f32[2,16,1024]{2,1,0:T(8,128)S(1)}, f...) custom-call(s32[1]{0:T(128)} %bitcast.1.me_ref, ...), custom_call_target="tpu_custom_call" | custom-call | flops 8589934592 | bytes 16777216 | tf_op jit(solution)/shard_map/compress/pallas_call | solution.py:253
  10.4 5.8 %compress.5 = (f32[2,16,1024]{2,1,0:T(8,128)S(1)}, f32[2,16,1024]{2,1,0:T(8,128)S(1)}, f32[2,16,1024]{2,1,0:T(8,128)S(1)}, f32[2,16,1024]{2,1,0:T(8,128)S(1)}, f32[38,1024]{1,0:T(8,128)S(1)}) custom-call(s32[1]{0:T(128)} %bitcast.1.me_ref, bf16[2,1024,4096]{2,1,0:T(8,128)(2,1)S(1)} %get-tuple-element.47.x_ref, f32[2,32,128]{2,1,0:T(8,128)S(1)} %get-tuple-element.48.g_ref, ...), custom_call_target="tpu_custom_call" | custom-call | flops 8589934592 | bytes 16777216 | tf_op jit(solution)/shard_map/compress/pallas_call | solution.py:301
  16.2 1.6 %collective-permute-start.3 = (f32[2,16,1024]{2,1,0:T(8,128)S(1)}, f32[2,16,1024]{2,1,0:T(8,128)S(1)}, u32[]{:S(2)}, u32[]{:S(2)}) collective-permute-start(f32[2,16,1024]{2,1,0:T(8,128)S(1)} %get-tuple-element.51), channel_id=1, source_target_pairs={{0,1},{1,2},{2,3},{3,0},{4,5},{5,6},{6,7},{7,4},{8,9},{9,10},{10,1... | collective-permute-start | bytes 393224 | tf_op jit(solution)/shard_map/ppermute | solution.py:654
  17.9 1.2 collective-permute-start.4
  19.1 1.8 %collective-permute-start.5 = (f32[2,16,1024]{2,1,0:T(8,128)S(1)}, f32[2,16,1024]{2,1,0:T(8,128)S(1)}, u32[]{:S(2)}, u32[]{:S(2)}) collective-permute-start(f32[2,16,1024]{2,1,0:T(8,128)S(1)} %get-tuple-element.53), channel_id=1, source_target_pairs={{0,3},{1,0},{2,1},{3,2},{4,7},{5,4},{6,5},{7,6},{8,11},{9,8},{10,9... | collective-permute-start | bytes 393224 | tf_op jit(solution)/shard_map/ppermute | solution.py:654
  20.9 1.3 %collective-permute-start.10 = (f32[38,1024]{1,0:T(8,128)S(1)}, f32[38,1024]{1,0:T(8,128)S(1)}, u32[]{:S(2)}, u32[]{:S(2)}) collective-permute-start(f32[38,1024]{1,0:T(8,128)S(1)} %get-tuple-element.59.refs_4_), channel_id=1, source_target_pairs={{3,1},{7,5},{11,9},{15,13},{19,17},{23,21},{27,25},{31,29}} | collective-permute-start | bytes 466952 | tf_op jit(solution)/shard_map/ppermute | solution.py:717
  22.2 1.3 %collective-permute-start.11 = (f32[38,1024]{1,0:T(8,128)S(1)}, f32[38,1024]{1,0:T(8,128)S(1)}, u32[]{:S(2)}, u32[]{:S(2)}) collective-permute-start(f32[38,1024]{1,0:T(8,128)S(1)} %get-tuple-element.59.refs_4_), channel_id=1, source_target_pairs={{2,1},{6,5},{10,9},{14,13},{18,17},{22,21},{26,25},{30,29}} | collective-permute-start | bytes 466952 | tf_op jit(solution)/shard_map/ppermute | solution.py:717
  23.5 3.7 %collective-permute-done.3.refs_5_ = f32[2,16,1024]{2,1,0:T(8,128)S(1)} collective-permute-done((f32[2,16,1024]{2,1,0:T(8,128)S(1)}, f32[2,16,1024]{2,1,0:T(8,128)S(1)}, u32[]{:S(2)}, u32[]{:S(2)}) %collective-permute-start.3) | collective-permute-done | bytes 131104 | tf_op jit(solution)/shard_map/ppermute | solution.py:654
  27.2 2.7 %collective-permute-start = (f32[2,16,1024]{2,1,0:T(8,128)S(1)}, f32[2,16,1024]{2,1,0:T(8,128)S(1)}, u32[]{:S(2)}, u32[]{:S(2)}) collective-permute-start(f32[2,16,1024]{2,1,0:T(8,128)S(1)} %get-tuple-element.44), channel_id=1, source_target_pairs={{0,1},{1,2},{2,3},{3,0},{4,5},{5,6},{6,7},{7,4},{8,9},{9,10},{10,1... | collective-permute-start | bytes 393224 | tf_op jit(solution)/shard_map/ppermute | solution.py:654
  29.8 0.3 collective-permute-done.4.refs_6_
  30.2 3.4 %collective-permute-start.1 = (f32[2,16,1024]{2,1,0:T(8,128)S(1)}, f32[2,16,1024]{2,1,0:T(8,128)S(1)}, u32[]{:S(2)}, u32[]{:S(2)}) collective-permute-start(f32[2,16,1024]{2,1,0:T(8,128)S(1)} %get-tuple-element.45), channel_id=1, source_target_pairs={{0,2},{1,3},{2,0},{3,1},{4,6},{5,7},{6,4},{7,5},{8,10},{9,11},{10,... | collective-permute-start | bytes 393224 | tf_op jit(solution)/shard_map/ppermute | solution.py:654
  33.6 6.5 %collective-permute-done.5.refs_7_ = f32[2,16,1024]{2,1,0:T(8,128)S(1)} collective-permute-done((f32[2,16,1024]{2,1,0:T(8,128)S(1)}, f32[2,16,1024]{2,1,0:T(8,128)S(1)}, u32[]{:S(2)}, u32[]{:S(2)}) %collective-permute-start.5) | collective-permute-done | bytes 131104 | tf_op jit(solution)/shard_map/ppermute | solution.py:654
  40.0 0.0 collective-permute-start.2
  40.0 10.9 %compress.6 = (f32[2,32,1024]{2,1,0:T(8,128)S(1)}, f32[2,32,1024]{2,1,0:T(8,128)S(1)}, f32[2,32,1024]{2,1,0:T(8,128)S(1)}, f32[2,32,1024]{2,1,0:T(8,128)S(1)}) custom-call(s32[1]{0:T(128)} %bitcast.1.me_ref, bf16[2,1024,4096]{2,1,0:T(8,128)(2,1)S(1)} %get-tuple-element.47.x_ref, f32[2,32,128]{2,1,0:T(8,128)S(1)} %get-tuple-element.48.g_ref, ...), custom_call_target="tpu_custom_call" | custom-call | flops 17179869184 | bytes 16777216 | tf_op jit(solution)/shard_map/compress/pallas_call | solution.py:301
  51.0 0.8 dynamic-slice_bitcast_fusion.refs_8_.refs_4_
  51.7 1.3 %collective-permute-start.9 = (f32[38,1024]{1,0:T(8,128)S(1)}, f32[38,1024]{1,0:T(8,128)S(1)}, u32[]{:S(2)}, u32[]{:S(2)}) collective-permute-start(f32[38,1024]{1,0:T(8,128)S(1)} %get-tuple-element.59.refs_4_), channel_id=1, source_target_pairs={{0,1},{4,5},{8,9},{12,13},{16,17},{20,21},{24,25},{28,29}} | collective-permute-start | bytes 466952 | tf_op jit(solution)/shard_map/ppermute | solution.py:717
  53.0 1.6 %collective-permute-start.6 = (f32[2,32,1024]{2,1,0:T(8,128)S(1)}, f32[2,32,1024]{2,1,0:T(8,128)S(1)}, u32[]{:S(2)}, u32[]{:S(2)}) collective-permute-start(f32[2,32,1024]{2,1,0:T(8,128)S(1)} %get-tuple-element.56), channel_id=1, source_target_pairs={{0,1},{1,2},{2,3},{3,0},{4,5},{5,6},{6,7},{7,4},{8,9},{9,10},{10,1... | collective-permute-start | bytes 786440 | tf_op jit(solution)/shard_map/ppermute | solution.py:654
  54.7 3.6 %collective-permute-start.7 = (f32[2,32,1024]{2,1,0:T(8,128)S(1)}, f32[2,32,1024]{2,1,0:T(8,128)S(1)}, u32[]{:S(2)}, u32[]{:S(2)}) collective-permute-start(f32[2,32,1024]{2,1,0:T(8,128)S(1)} %get-tuple-element.57), channel_id=1, source_target_pairs={{0,2},{1,3},{2,0},{3,1},{4,6},{5,7},{6,4},{7,5},{8,10},{9,11},{10,... | collective-permute-start | bytes 786440 | tf_op jit(solution)/shard_map/ppermute | solution.py:654
  58.3 1.1 doppler.3
  59.4 0.1 collective-permute-start.8
  59.5 3.4 %collective-permute-start.15 = (f32[1216,128]{1,0:T(8,128)S(1)}, f32[1216,128]{1,0:T(8,128)S(1)}, u32[]{:S(2)}, u32[]{:S(2)}) collective-permute-start(f32[1216,128]{1,0:T(8,128)S(1)} %get-tuple-element.69), channel_id=1, source_target_pairs={{1,0},{3,2},{5,4},{7,6},{9,8},{11,10},{13,12},{15,14},{17,16},{19,... | collective-permute-start | bytes 1867784 | tf_op jit(solution)/shard_map/ppermute | solution.py:696
  62.9 5.8 %copy-done.8 = bf16[2,1024,4096]{2,1,0:T(8,128)(2,1)S(1)} copy-done((bf16[2,1024,4096]{2,1,0:T(8,128)(2,1)S(1)}, bf16[2,1024,4096]{2,1,0:T(8,128)(2,1)}, u32[]{:S(2)}) %copy-start.8) | copy-done | bytes 16777240
  68.7 10.6 %compress.7 = (f32[2,32,1024]{2,1,0:T(8,128)S(1)}, f32[2,32,1024]{2,1,0:T(8,128)S(1)}, f32[2,32,1024]{2,1,0:T(8,128)S(1)}, f32[2,32,1024]{2,1,0:T(8,128)S(1)}) custom-call(s32[1]{0:T(128)} %bitcast.1.me_ref, bf16[2,1024,4096]{2,1,0:T(8,128)(2,1)S(1)} %copy-done.8, f32[2,32,128]{2,1,0:T(8,128)S(1)} %get-tuple-element.48.g_ref, ...), custom_call_target="tpu_custom_call" | custom-call | flops 17179869184 | bytes 16777216 | tf_op jit(solution)/shard_map/compress/pallas_call | solution.py:301
  79.2 0.0 copy-start.1
  79.2 0.0 copy-start.4
  79.3 0.1 collective-permute-start.12
  79.3 2.1 %collective-permute-start.13 = (f32[2,32,1024]{2,1,0:T(8,128)S(1)}, f32[2,32,1024]{2,1,0:T(8,128)S(1)}, u32[]{:S(2)}, u32[]{:S(2)}) collective-permute-start(f32[2,32,1024]{2,1,0:T(8,128)S(1)} %get-tuple-element.66), channel_id=1, source_target_pairs={{0,2},{1,3},{2,0},{3,1},{4,6},{5,7},{6,4},{7,5},{8,10},{9,11},{10,... | collective-permute-start | bytes 786440 | tf_op jit(solution)/shard_map/ppermute | solution.py:654
  81.4 1.9 %collective-permute-start.14 = (f32[2,32,1024]{2,1,0:T(8,128)S(1)}, f32[2,32,1024]{2,1,0:T(8,128)S(1)}, u32[]{:S(2)}, u32[]{:S(2)}) collective-permute-start(f32[2,32,1024]{2,1,0:T(8,128)S(1)} %get-tuple-element.67), channel_id=1, source_target_pairs={{0,3},{1,0},{2,1},{3,2},{4,7},{5,4},{6,5},{7,6},{8,11},{9,8},{10,9... | collective-permute-start | bytes 786440 | tf_op jit(solution)/shard_map/ppermute | solution.py:654
  84.7 0.1 broadcast_in_dim.8.fm_ref
  84.8 3.5 %phases.1 = (f32[2,32,40,128]{3,2,1,0:T(8,128)S(1)}, f32[2,32,56,128]{3,2,1,0:T(8,128)S(1)}, f32[256,128]{1,0:T(8,128)S(1)}) custom-call(f32[96,128]{1,0:T(8,128)S(1)} %broadcast_in_dim.8.fm_ref, f32[8,4096]{1,0:T(8,128)S(1)} %copy-done.2, f32[128,128]{1,0:T(8,128)S(1)} %copy-done.3), custom_call_target="tpu_custom_call" | custom-call | flops 23592960 | bytes 3145728 | tf_op jit(solution)/shard_map/phases/pallas_call | solution.py:460
  88.2 1.8 %doppler.4 = (f32[2,32,32,128]{3,2,1,0:T(8,128)S(1)}, f32[1216,128]{1,0:T(8,128)S(1)}) custom-call(f32[2,32,1024]{2,1,0:T(8,128)S(1)} %get-tuple-element.55.refs_0_.keep_ref, f32[2,32,1024]{2,1,0:T(8,128)S(1)} %collective-permute-done.6.refs_1_, f32[2,32,1024]{2,1,0:T(8,128)S(1)} %collective-permute-done.7.refs_2_, ...), custom_call_target="tpu_custom_call" | custom-call | flops 402653184 | bytes 2097152 | tf_op jit(solution)/shard_map/doppler/pallas_call | solution.py:384
  90.1 3.7 %focus.2 = (f32[2,40,4096]{2,1,0:T(8,128)S(1)}, f32[2,40,128]{2,1,0:T(8,128)S(1)}, f32[2,40,128]{2,1,0:T(8,128)S(1)}, f32[8,128]{1,0:T(8,128)S(1)}) custom-call(s32[96]{0:T(128)S(1)} %bitcast.5, s32[1]{0:T(128)} %bitcast.1.me_ref, f32[2,32,32,128]{3,2,1,0:T(8,128)S(1)} %get-tuple-element.54.refs_0_, ...), custom_call_target="tpu_custom_call" | custom-call | flops 503316480 | bytes 5242880 | tf_op jit(solution)/shard_map/focus/pallas_call | solution.py:566
  93.8 3.3 %collective-permute-done.12.refs_1_ = f32[2,32,1024]{2,1,0:T(8,128)S(1)} collective-permute-done((f32[2,32,1024]{2,1,0:T(8,128)S(1)}, f32[2,32,1024]{2,1,0:T(8,128)S(1)}, u32[]{:S(2)}, u32[]{:S(2)}) %collective-permute-start.12) | collective-permute-done | bytes 262176 | tf_op jit(solution)/shard_map/ppermute | solution.py:654
  97.1 4.2 %collective-permute-done.13.refs_2_ = f32[2,32,1024]{2,1,0:T(8,128)S(1)} collective-permute-done((f32[2,32,1024]{2,1,0:T(8,128)S(1)}, f32[2,32,1024]{2,1,0:T(8,128)S(1)}, u32[]{:S(2)}, u32[]{:S(2)}) %collective-permute-start.13) | collective-permute-done | bytes 262176 | tf_op jit(solution)/shard_map/ppermute | solution.py:654
  101.3 3.1 %collective-permute-done.14.refs_3_ = f32[2,32,1024]{2,1,0:T(8,128)S(1)} collective-permute-done((f32[2,32,1024]{2,1,0:T(8,128)S(1)}, f32[2,32,1024]{2,1,0:T(8,128)S(1)}, u32[]{:S(2)}, u32[]{:S(2)}) %collective-permute-start.14) | collective-permute-done | bytes 262176 | tf_op jit(solution)/shard_map/ppermute | solution.py:654
  104.4 1.0 doppler.5.refs_1_
  105.5 4.8 %focus.3 = (f32[2,56,4096]{2,1,0:T(8,128)S(1)}, f32[2,56,128]{2,1,0:T(8,128)S(1)}, f32[2,96,128]{2,1,0:T(8,128)S(1)}, f32[8,128]{1,0:T(8,128)S(1)}) custom-call(s32[96]{0:T(128)S(1)} %bitcast.6, s32[1]{0:T(128)} %bitcast.1.me_ref, f32[2,32,32,128]{3,2,1,0:T(8,128)S(1)} %get-tuple-element.61.refs_1_.refs_0_, f32[2,32,32,128]{3,2,1,0:T(8,128)S(1)} %doppler.5.refs_1_, ...), custom_call_target="tpu_custom_call" | custom-call | flops 704643072 | bytes 7340032 | tf_op jit(solution)/shard_map/focus/pallas_call | solution.py:566
  110.2 1.9 %collective-permute-start.16 = (f32[2,96,128]{2,1,0:T(8,128)S(1)}, f32[2,96,128]{2,1,0:T(8,128)S(1)}, u32[]{:S(2)}, u32[]{:S(2)}) collective-permute-start(f32[2,96,128]{2,1,0:T(8,128)S(1)} %get-tuple-element.76), channel_id=1, source_target_pairs={{0,4},{4,8},{8,12},{12,16},{16,20},{20,24},{24,28},{1,5},{5,9},{9,... | collective-permute-start | bytes 294920 | tf_op jit(solution)/shard_map/ppermute | solution.py:750
  112.2 0.1 pad_add_fusion.seam_ref
  112.2 4.8 %collective-permute-done.16.refs_2_ = f32[2,96,128]{2,1,0:T(8,128)S(1)} collective-permute-done((f32[2,96,128]{2,1,0:T(8,128)S(1)}, f32[2,96,128]{2,1,0:T(8,128)S(1)}, u32[]{:S(2)}, u32[]{:S(2)}) %collective-permute-start.16) | collective-permute-done | bytes 98336 | tf_op jit(solution)/shard_map/ppermute | solution.py:750
  117.1 0.6 blend.1
  117.7 1.9 %collective-permute-start.17 = (f32[8,128]{1,0:T(8,128)S(1)}, f32[8,128]{1,0:T(8,128)S(1)}, u32[]{:S(2)}, u32[]{:S(2)}) collective-permute-start(f32[8,128]{1,0:T(8,128)S(1)} %get-tuple-element.80.refs_4_), channel_id=1, source_target_pairs={{0,1},{1,2},{2,3},{3,0},{4,5},{5,6},{6,7},{7,4},{8,9},{9,10},{10,1... | collective-permute-start | bytes 12296 | tf_op jit(solution)/shard_map/ppermute | solution.py:654
  119.6 2.3 %collective-permute-start.18 = (f32[8,128]{1,0:T(8,128)S(1)}, f32[8,128]{1,0:T(8,128)S(1)}, u32[]{:S(2)}, u32[]{:S(2)}) collective-permute-start(f32[8,128]{1,0:T(8,128)S(1)} %get-tuple-element.80.refs_4_), channel_id=1, source_target_pairs={{0,2},{1,3},{2,0},{3,1},{4,6},{5,7},{6,4},{7,5},{8,10},{9,11},{10,... | collective-permute-start | bytes 12296 | tf_op jit(solution)/shard_map/ppermute | solution.py:654
  121.9 2.2 %collective-permute-done.18.refs_6_ = f32[8,128]{1,0:T(8,128)S(1)} collective-permute-done((f32[8,128]{1,0:T(8,128)S(1)}, f32[8,128]{1,0:T(8,128)S(1)}, u32[]{:S(2)}, u32[]{:S(2)}) %collective-permute-start.18) | collective-permute-done | bytes 4128 | tf_op jit(solution)/shard_map/ppermute | solution.py:654
  124.1 1.4 %collective-permute-done.19.refs_7_ = f32[8,128]{1,0:T(8,128)S(1)} collective-permute-done((f32[8,128]{1,0:T(8,128)S(1)}, f32[8,128]{1,0:T(8,128)S(1)}, u32[]{:S(2)}, u32[]{:S(2)}) %collective-permute-start.19) | collective-permute-done | bytes 4128 | tf_op jit(solution)/shard_map/ppermute | solution.py:654
  125.5 1.6 %finish.1 = bf16[1,2,96,4096]{3,2,1,0:T(8,128)(2,1)} custom-call(f32[2,40,4096]{2,1,0:T(8,128)S(1)} %get-tuple-element.63.refs_0_, f32[2,56,4096]{2,1,0:T(8,128)S(1)} %get-tuple-element.73.refs_1_, f32[2,40,128]{2,1,0:T(8,128)S(1)} %get-tuple-element.78.refs_2_, f32[2,56,128]{2,1,0:T(8,128)S(1)} %get-tuple-element.79.refs_3_, ...), custom_call_target="tpu_custom_call" | custom-call | tf_op jit(solution)/shard_map/finish/pallas_call | solution.py:643
  (27 shorter events, 0.1 us)
Async XLA Ops:
  0.0 0.8 copy-start.5
  0.8 1.0 copy-start.6
  10.4 29.6 %copy-start.7 = (bf16[2,1024,4096]{2,1,0:T(8,128)(2,1)}, bf16[2,1024,4096]{2,1,0:T(8,128)(2,1)S(1)}, u32[]{:S(2)}) copy-start(bf16[2,1024,4096]{2,1,0:T(8,128)(2,1)S(1)} %get-tuple-element.47.x_ref) | copy-start | bytes 50331652
  16.2 10.9 %collective-permute-start.3 = (f32[2,16,1024]{2,1,0:T(8,128)S(1)}, f32[2,16,1024]{2,1,0:T(8,128)S(1)}, u32[]{:S(2)}, u32[]{:S(2)}) collective-permute-start(f32[2,16,1024]{2,1,0:T(8,128)S(1)} %get-tuple-element.51), channel_id=1, source_target_pairs={{0,1},{1,2},{2,3},{3,0},{4,5},{5,6},{6,7},{7,4},{8,9},{9,10},{10,1... | collective-permute-start | bytes 393224 | tf_op jit(solution)/shard_map/ppermute | solution.py:654
  17.9 12.3 %collective-permute-start.4 = (f32[2,16,1024]{2,1,0:T(8,128)S(1)}, f32[2,16,1024]{2,1,0:T(8,128)S(1)}, u32[]{:S(2)}, u32[]{:S(2)}) collective-permute-start(f32[2,16,1024]{2,1,0:T(8,128)S(1)} %get-tuple-element.52), channel_id=1, source_target_pairs={{0,2},{1,3},{2,0},{3,1},{4,6},{5,7},{6,4},{7,5},{8,10},{9,11},{10,... | collective-permute-start | bytes 393224 | tf_op jit(solution)/shard_map/ppermute | solution.py:654
  19.1 20.9 %collective-permute-start.5 = (f32[2,16,1024]{2,1,0:T(8,128)S(1)}, f32[2,16,1024]{2,1,0:T(8,128)S(1)}, u32[]{:S(2)}, u32[]{:S(2)}) collective-permute-start(f32[2,16,1024]{2,1,0:T(8,128)S(1)} %get-tuple-element.53), channel_id=1, source_target_pairs={{0,3},{1,0},{2,1},{3,2},{4,7},{5,4},{6,5},{7,6},{8,11},{9,8},{10,9... | collective-permute-start | bytes 393224 | tf_op jit(solution)/shard_map/ppermute | solution.py:654
  20.9 38.5 %collective-permute-start.10 = (f32[38,1024]{1,0:T(8,128)S(1)}, f32[38,1024]{1,0:T(8,128)S(1)}, u32[]{:S(2)}, u32[]{:S(2)}) collective-permute-start(f32[38,1024]{1,0:T(8,128)S(1)} %get-tuple-element.59.refs_4_), channel_id=1, source_target_pairs={{3,1},{7,5},{11,9},{15,13},{19,17},{23,21},{27,25},{31,29}} | collective-permute-start | bytes 466952 | tf_op jit(solution)/shard_map/ppermute | solution.py:717
  22.2 37.3 %collective-permute-start.11 = (f32[38,1024]{1,0:T(8,128)S(1)}, f32[38,1024]{1,0:T(8,128)S(1)}, u32[]{:S(2)}, u32[]{:S(2)}) collective-permute-start(f32[38,1024]{1,0:T(8,128)S(1)} %get-tuple-element.59.refs_4_), channel_id=1, source_target_pairs={{2,1},{6,5},{10,9},{14,13},{18,17},{22,21},{26,25},{30,29}} | collective-permute-start | bytes 466952 | tf_op jit(solution)/shard_map/ppermute | solution.py:717
  27.2 24.6 %collective-permute-start = (f32[2,16,1024]{2,1,0:T(8,128)S(1)}, f32[2,16,1024]{2,1,0:T(8,128)S(1)}, u32[]{:S(2)}, u32[]{:S(2)}) collective-permute-start(f32[2,16,1024]{2,1,0:T(8,128)S(1)} %get-tuple-element.44), channel_id=1, source_target_pairs={{0,1},{1,2},{2,3},{3,0},{4,5},{5,6},{6,7},{7,4},{8,9},{9,10},{10,1... | collective-permute-start | bytes 393224 | tf_op jit(solution)/shard_map/ppermute | solution.py:654
  30.2 22.9 %collective-permute-start.1 = (f32[2,16,1024]{2,1,0:T(8,128)S(1)}, f32[2,16,1024]{2,1,0:T(8,128)S(1)}, u32[]{:S(2)}, u32[]{:S(2)}) collective-permute-start(f32[2,16,1024]{2,1,0:T(8,128)S(1)} %get-tuple-element.45), channel_id=1, source_target_pairs={{0,2},{1,3},{2,0},{3,1},{4,6},{5,7},{6,4},{7,5},{8,10},{9,11},{10,... | collective-permute-start | bytes 393224 | tf_op jit(solution)/shard_map/ppermute | solution.py:654
  40.0 14.7 %collective-permute-start.2 = (f32[2,16,1024]{2,1,0:T(8,128)S(1)}, f32[2,16,1024]{2,1,0:T(8,128)S(1)}, u32[]{:S(2)}, u32[]{:S(2)}) collective-permute-start(f32[2,16,1024]{2,1,0:T(8,128)S(1)} %get-tuple-element.46), channel_id=1, source_target_pairs={{0,3},{1,0},{2,1},{3,2},{4,7},{5,4},{6,5},{7,6},{8,11},{9,8},{10,9... | collective-permute-start | bytes 393224 | tf_op jit(solution)/shard_map/ppermute | solution.py:654
  40.0 18.3 %copy-start = (bf16[512,256]{1,0:T(8,128)(2,1)S(1)}, bf16[512,256]{1,0:T(8,128)(2,1)}, u32[]{:S(2)}) copy-start(bf16[512,256]{1,0:T(8,128)(2,1)} %constant.22.clone.refs_9_.refs_5_.refs_7_) | copy-start | bytes 786436
  51.7 27.5 %collective-permute-start.9 = (f32[38,1024]{1,0:T(8,128)S(1)}, f32[38,1024]{1,0:T(8,128)S(1)}, u32[]{:S(2)}, u32[]{:S(2)}) collective-permute-start(f32[38,1024]{1,0:T(8,128)S(1)} %get-tuple-element.59.refs_4_), channel_id=1, source_target_pairs={{0,1},{4,5},{8,9},{12,13},{16,17},{20,21},{24,25},{28,29}} | collective-permute-start | bytes 466952 | tf_op jit(solution)/shard_map/ppermute | solution.py:717
  53.0 26.3 %collective-permute-start.6 = (f32[2,32,1024]{2,1,0:T(8,128)S(1)}, f32[2,32,1024]{2,1,0:T(8,128)S(1)}, u32[]{:S(2)}, u32[]{:S(2)}) collective-permute-start(f32[2,32,1024]{2,1,0:T(8,128)S(1)} %get-tuple-element.56), channel_id=1, source_target_pairs={{0,1},{1,2},{2,3},{3,0},{4,5},{5,6},{6,7},{7,4},{8,9},{9,10},{10,1... | collective-permute-start | bytes 786440 | tf_op jit(solution)/shard_map/ppermute | solution.py:654
  54.7 26.7 %collective-permute-start.7 = (f32[2,32,1024]{2,1,0:T(8,128)S(1)}, f32[2,32,1024]{2,1,0:T(8,128)S(1)}, u32[]{:S(2)}, u32[]{:S(2)}) collective-permute-start(f32[2,32,1024]{2,1,0:T(8,128)S(1)} %get-tuple-element.57), channel_id=1, source_target_pairs={{0,2},{1,3},{2,0},{3,1},{4,6},{5,7},{6,4},{7,5},{8,10},{9,11},{10,... | collective-permute-start | bytes 786440 | tf_op jit(solution)/shard_map/ppermute | solution.py:654
  59.4 28.8 %collective-permute-start.8 = (f32[2,32,1024]{2,1,0:T(8,128)S(1)}, f32[2,32,1024]{2,1,0:T(8,128)S(1)}, u32[]{:S(2)}, u32[]{:S(2)}) collective-permute-start(f32[2,32,1024]{2,1,0:T(8,128)S(1)} %get-tuple-element.58), channel_id=1, source_target_pairs={{0,3},{1,0},{2,1},{3,2},{4,7},{5,4},{6,5},{7,6},{8,11},{9,8},{10,9... | collective-permute-start | bytes 786440 | tf_op jit(solution)/shard_map/ppermute | solution.py:654
  59.5 46.0 %collective-permute-start.15 = (f32[1216,128]{1,0:T(8,128)S(1)}, f32[1216,128]{1,0:T(8,128)S(1)}, u32[]{:S(2)}, u32[]{:S(2)}) collective-permute-start(f32[1216,128]{1,0:T(8,128)S(1)} %get-tuple-element.69), channel_id=1, source_target_pairs={{1,0},{3,2},{5,4},{7,6},{9,8},{11,10},{13,12},{15,14},{17,16},{19,... | collective-permute-start | bytes 1867784 | tf_op jit(solution)/shard_map/ppermute | solution.py:696
  62.9 5.8 %copy-start.8 = (bf16[2,1024,4096]{2,1,0:T(8,128)(2,1)S(1)}, bf16[2,1024,4096]{2,1,0:T(8,128)(2,1)}, u32[]{:S(2)}) copy-start(bf16[2,1024,4096]{2,1,0:T(8,128)(2,1)} %copy-done.7) | copy-start | bytes 50331652
  68.7 16.0 %copy-start.9 = (f32[1,96]{1,0:T(1,128)S(1)}, f32[1,96]{1,0:T(1,128)}, u32[]{:S(2)}) copy-start(f32[1,96]{1,0:T(1,128)} %param.15) | copy-start | bytes 1156
  68.7 16.1 %copy-start.2 = (f32[8,4096]{1,0:T(8,128)S(1)}, f32[8,4096]{1,0:T(8,128)}, u32[]{:S(2)}) copy-start(f32[8,4096]{1,0:T(8,128)} %w_ref.1) | copy-start | bytes 393220
  68.7 16.1 %copy-start.3 = (f32[128,128]{1,0:T(8,128)S(1)}, f32[128,128]{1,0:T(8,128)}, u32[]{:S(2)}) copy-start(f32[128,128]{1,0:T(8,128)} %constant.23.clone.pick_ref) | copy-start | bytes 196612
  79.2 10.9 %copy-start.1 = (f32[2,32,128]{2,1,0:T(8,128)S(1)}, f32[2,32,128]{2,1,0:T(8,128)}, u32[]{:S(2)}) copy-start(f32[2,32,128]{2,1,0:T(8,128)} %constant.24.clone.refs_4_.refs_6_) | copy-start | bytes 98308
  79.2 10.9 %copy-start.4 = (s32[1,96]{1,0:T(1,128)S(1)}, s32[1,96]{1,0:T(1,128)}, u32[]{:S(2)}) copy-start(s32[1,96]{1,0:T(1,128)} %param.16) | copy-start | bytes 1156
  79.3 17.8 %collective-permute-start.12 = (f32[2,32,1024]{2,1,0:T(8,128)S(1)}, f32[2,32,1024]{2,1,0:T(8,128)S(1)}, u32[]{:S(2)}, u32[]{:S(2)}) collective-permute-start(f32[2,32,1024]{2,1,0:T(8,128)S(1)} %get-tuple-element.65), channel_id=1, source_target_pairs={{0,1},{1,2},{2,3},{3,0},{4,5},{5,6},{6,7},{7,4},{8,9},{9,10},{10,1... | collective-permute-start | bytes 786440 | tf_op jit(solution)/shard_map/ppermute | solution.py:654
  79.3 22.0 %collective-permute-start.13 = (f32[2,32,1024]{2,1,0:T(8,128)S(1)}, f32[2,32,1024]{2,1,0:T(8,128)S(1)}, u32[]{:S(2)}, u32[]{:S(2)}) collective-permute-start(f32[2,32,1024]{2,1,0:T(8,128)S(1)} %get-tuple-element.66), channel_id=1, source_target_pairs={{0,2},{1,3},{2,0},{3,1},{4,6},{5,7},{6,4},{7,5},{8,10},{9,11},{10,... | collective-permute-start | bytes 786440 | tf_op jit(solution)/shard_map/ppermute | solution.py:654
  81.4 23.0 %collective-permute-start.14 = (f32[2,32,1024]{2,1,0:T(8,128)S(1)}, f32[2,32,1024]{2,1,0:T(8,128)S(1)}, u32[]{:S(2)}, u32[]{:S(2)}) collective-permute-start(f32[2,32,1024]{2,1,0:T(8,128)S(1)} %get-tuple-element.67), channel_id=1, source_target_pairs={{0,3},{1,0},{2,1},{3,2},{4,7},{5,4},{6,5},{7,6},{8,11},{9,8},{10,9... | collective-permute-start | bytes 786440 | tf_op jit(solution)/shard_map/ppermute | solution.py:654
  110.2 6.8 %collective-permute-start.16 = (f32[2,96,128]{2,1,0:T(8,128)S(1)}, f32[2,96,128]{2,1,0:T(8,128)S(1)}, u32[]{:S(2)}, u32[]{:S(2)}) collective-permute-start(f32[2,96,128]{2,1,0:T(8,128)S(1)} %get-tuple-element.76), channel_id=1, source_target_pairs={{0,4},{4,8},{8,12},{12,16},{16,20},{20,24},{24,28},{1,5},{5,9},{9,... | collective-permute-start | bytes 294920 | tf_op jit(solution)/shard_map/ppermute | solution.py:750
  117.7 4.2 %collective-permute-start.17 = (f32[8,128]{1,0:T(8,128)S(1)}, f32[8,128]{1,0:T(8,128)S(1)}, u32[]{:S(2)}, u32[]{:S(2)}) collective-permute-start(f32[8,128]{1,0:T(8,128)S(1)} %get-tuple-element.80.refs_4_), channel_id=1, source_target_pairs={{0,1},{1,2},{2,3},{3,0},{4,5},{5,6},{6,7},{7,4},{8,9},{9,10},{10,1... | collective-permute-start | bytes 12296 | tf_op jit(solution)/shard_map/ppermute | solution.py:654
  119.6 4.5 %collective-permute-start.18 = (f32[8,128]{1,0:T(8,128)S(1)}, f32[8,128]{1,0:T(8,128)S(1)}, u32[]{:S(2)}, u32[]{:S(2)}) collective-permute-start(f32[8,128]{1,0:T(8,128)S(1)} %get-tuple-element.80.refs_4_), channel_id=1, source_target_pairs={{0,2},{1,3},{2,0},{3,1},{4,6},{5,7},{6,4},{7,5},{8,10},{9,11},{10,... | collective-permute-start | bytes 12296 | tf_op jit(solution)/shard_map/ppermute | solution.py:654
  121.9 3.6 %collective-permute-start.19 = (f32[8,128]{1,0:T(8,128)S(1)}, f32[8,128]{1,0:T(8,128)S(1)}, u32[]{:S(2)}, u32[]{:S(2)}) collective-permute-start(f32[8,128]{1,0:T(8,128)S(1)} %get-tuple-element.80.refs_4_), channel_id=1, source_target_pairs={{0,3},{1,0},{2,1},{3,2},{4,7},{5,4},{6,5},{7,6},{8,11},{9,8},{10,9... | collective-permute-start | bytes 12296 | tf_op jit(solution)/shard_map/ppermute | solution.py:654

commit v3 on v2

--- a/solution.py
+++ b/solution.py
@@ -277,7 +277,7 @@
     lines, samples = x.shape[1], x.shape[2]
     columns = samples // LANES
     width = 2 * count * rows
-    mblk = min(512, lines)
+    mblk = min(1024 if rows <= 16 else 512, lines)
     again = start < MARGIN <= start + rows
 
     def kernel(me_ref, x_ref, g_ref, keep_ref, *refs):
@@ -315,7 +315,7 @@
     )(me, x, g, keep)
 
 
-def doppler(chunks, flat, tw, matrix, lead, after):
+def doppler(chunks, flat, me, tw, matrix, lead, after):
     count = len(chunks[0])
     lines = chunks[0][0].shape[2]
     sizes = [pieces[0].shape[1] for pieces in chunks]
@@ -325,8 +325,9 @@
     number = count * len(chunks) + len(flat)
     total = rows + (HALO if flat else 0)
 
-    def kernel(*refs):
+    def kernel(me_ref, *refs):
         tw_ref, mat_ref = refs[number:number + 2]
+        own_tw = tw_ref.at[me_ref[0]]
         outs, scratch = refs[number + 2 + len(after):-1], refs[-1]
         out_ref = outs[0]
 
@@ -341,8 +342,8 @@
             for k0 in range(count):
                 for k1, (vr, vi) in enumerate(dft_list(inner[k0], -1)):
                     k = k0 + count * k1
-                    tr = tw_ref[0, k:k + 1, :]
-                    ti = tw_ref[1, k:k + 1, :]
+                    tr = own_tw[0, k:k + 1, :]
+                    ti = own_tw[1, k:k + 1, :]
                     scratch[place(k), :LANES] = vr * tr - vi * ti
                     scratch[place(k), LANES:] = vr * ti + vi * tr
 
@@ -383,7 +384,7 @@
 
     return pl.pallas_call(
         kernel,
-        in_specs=[VMEM] * (number + 2) + [ANY] * len(after),
+        in_specs=[pl.BlockSpec(memory_space=pltpu.SMEM)] + [VMEM] * (number + 2) + [ANY] * len(after),
         out_shape=[jax.ShapeDtypeStruct((2, columns, rows, LANES), F32)]
         + [jax.ShapeDtypeStruct((2 * columns * MARGIN, LANES), F32)] * ((lead > 0) + (len(flat) > 0)),
         compiler_params=pltpu.CompilerParams(vmem_limit_bytes=(4 + total // 5) * 2**20),
@@ -391,7 +392,7 @@
         cost_estimate=pl.CostEstimate(
             flops=2 * columns * rows * 256 * 768, bytes_accessed=16 * columns * rows * LANES, transcendentals=0),
         name="doppler",
-    )(*[piece for pieces in chunks for piece in pieces], *flat, tw, matrix, *after)
+    )(me, *[piece for pieces in chunks for piece in pieces], *flat, tw, matrix, *after)
 
 
 def turn_pair(turns):
@@ -656,7 +657,7 @@
 
 def plan(per):
     if per == 96:
-        return [16, 16, 32, 32], [[0, 1], [2], [3]], [40, 56]
+        return [16, 16, 32, 32], [[0, 1], [2], [3]], [40, 32, 24]
     return [per], [[0]], [per]
 
 
@@ -674,7 +675,6 @@
     tw_all = np.stack([
         turn[0][:, :, None] * base[0] - turn[1][:, :, None] * base[1],
         turn[0][:, :, None] * base[1] + turn[1][:, :, None] * base[0]], axis=1).astype(np.float32)
-    tw_forward = lax.dynamic_index_in_dim(jnp.asarray(tw_all), me, 0, keepdims=False)
     tw_inverse = column_twiddle(columns, length, 1, 1.0 / length)
     matrix = lane_matrix()
 
@@ -688,7 +688,7 @@
     def azimuth(flat, after):
         n = len(dop)
         lead = MARGIN if n == 0 else 0
-        outs = doppler([chunks[c] for c in groups[n]], flat, tw_forward, matrix, lead, after)
+        outs = doppler([chunks[c] for c in groups[n]], flat, me1, tw_all, matrix, lead, after)
         dop.append(outs[0])
         blocks.append((starts[groups[n][0]], outs[0].shape[2]))
         if lead:

time: 128 us -> 127 us (level)
  local copies, waits for them, and re-layouts: 8.36 us -> 1.84 us
  waiting for transfers between devices: 29.6 us -> 36.1 us
  starting transfers between devices: 33.5 us -> 32.1 us
    ppermute x15, waiting for transfers between devices: 24.7 us -> 31.3 us  [cyclic(): lax.ppermute(value, axis, [(i, (i + steps) % count) for i in range(count)])]
    unnamed x20 -> x18, local copies, waits for them, and re-layouts: 7.52 us -> 1.77 us
    ppermute x15, starting transfers between devices: 24.3 us -> 22.9 us  [cyclic(): lax.ppermute(value, axis, [(i, (i + steps) % count) for i in range(count)])]
    pallas_call x2 -> x3, Pallas kernels: 8.41 us -> 9.7 us  [focus_rows(): pl.pallas_call(kernel, in_specs=[pl.BlockSpec(memory_space=pltpu.SMEM)] *...]
  transfers between devices with their start and end apart: 20 -> 20, of which waited for: 9 -> 10; matrix products, arithmetic and copies ran while one was open for 1% -> 0% of each run, Pallas kernels for 26% -> 29%
where the time goes in v3:
time: 127 us; the launch traced here: 126 us
  Pallas kernels  54.8 us (43%)
  waiting for transfers between devices  36.1 us (28%)
  starting transfers between devices  32.1 us (25%)
  local copies, waits for them, and re-layouts  1.84 us (1%)
  between operations  1.57 us (1%)
    ppermute x15, waiting for transfers between devices, cyclic(): lax.ppermute(value, axis, [(i, (i + steps) % count) for i in range(count)])  31.3 us
    pallas_call x3, Pallas kernels, compress(): pl.pallas_call(kernel, in_specs=[pl.BlockSpec(memory_space=pltpu.SMEM), V...  26.7 us
    ppermute x15, starting transfers between devices, cyclic(): lax.ppermute(value, axis, [(i, (i + steps) % count) for i in range(count)])  22.9 us
    pallas_call x3, Pallas kernels, focus_rows(): pl.pallas_call(kernel, in_specs=[pl.BlockSpec(memory_space=pltpu.SMEM)] *...  9.7 us
    pallas_call x1, Pallas kernels, compress_first(): pl.pallas_call(kernel, in_specs=[pl.BlockSpec(memory_space=pltpu.SMEM), h...  8.67 us
    ppermute x1, waiting for transfers between devices, strip(): lax.ppermute(tails[-1], 'chip', [(j, j + 1) for j in range(chips - 1)])  4.83 us
    pallas_call x3, Pallas kernels, doppler(): pl.pallas_call(kernel, in_specs=[pl.BlockSpec(memory_space=pltpu.SMEM)] +...  4.01 us
    ppermute x3, starting transfers between devices, strip(): raw.append(lax.ppermute(outs[count], 'line', [((mid - s) % count, mid)]))  3.86 us
  transfers between devices with their start and end apart: 20, of which 10 were waited for; matrix products, arithmetic and copies ran while one was open for 0% of the time, Pallas kernels for 29%

profile of v3, /device:TPU:12, one launch (start us, length us, event | category | flops | bytes accessed | tf_op | source)
XLA Modules:
  0.0 126.5 jit_solution(15064683720634337227)
XLA Ops:
  0.0 0.8 copy-done.6
  0.8 1.0 copy-done.7
  1.7 8.7 %compress.4 = (f32[2,16,1024]{2,1,0:T(8,128)S(1)}, f32[2,16,1024]{2,1,0:T(8,128)S(1)}, f32[2,16,1024]{2,1,0:T(8,128)S(1)}, f32[2,16,1024]{2,1,0:T(8,128)S(1)}, f...) custom-call(s32[1]{0:T(128)} %bitcast.1.me_ref, ...), custom_call_target="tpu_custom_call" | custom-call | flops 8589934592 | bytes 16777216 | tf_op jit(solution)/shard_map/compress/pallas_call | solution.py:253
  10.4 4.8 %compress.5 = (f32[2,16,1024]{2,1,0:T(8,128)S(1)}, f32[2,16,1024]{2,1,0:T(8,128)S(1)}, f32[2,16,1024]{2,1,0:T(8,128)S(1)}, f32[2,16,1024]{2,1,0:T(8,128)S(1)}, f32[38,1024]{1,0:T(8,128)S(1)}) custom-call(s32[1]{0:T(128)} %bitcast.1.me_ref, bf16[2,1024,4096]{2,1,0:T(8,128)(2,1)S(1)} %get-tuple-element.53.x_ref, f32[2,32,128]{2,1,0:T(8,128)S(1)} %get-tuple-element.54.g_ref, ...), custom_call_target="tpu_custom_call" | custom-call | flops 8589934592 | bytes 16777216 | tf_op jit(solution)/shard_map/compress/pallas_call | solution.py:301
  15.3 1.6 %collective-permute-start.3 = (f32[2,16,1024]{2,1,0:T(8,128)S(1)}, f32[2,16,1024]{2,1,0:T(8,128)S(1)}, u32[]{:S(2)}, u32[]{:S(2)}) collective-permute-start(f32[2,16,1024]{2,1,0:T(8,128)S(1)} %get-tuple-element.57), channel_id=1, source_target_pairs={{0,1},{1,2},{2,3},{3,0},{4,5},{5,6},{6,7},{7,4},{8,9},{9,10},{10,1... | collective-permute-start | bytes 393224 | tf_op jit(solution)/shard_map/ppermute | solution.py:655
  16.9 1.2 collective-permute-start.4
  18.1 1.8 %collective-permute-start.5 = (f32[2,16,1024]{2,1,0:T(8,128)S(1)}, f32[2,16,1024]{2,1,0:T(8,128)S(1)}, u32[]{:S(2)}, u32[]{:S(2)}) collective-permute-start(f32[2,16,1024]{2,1,0:T(8,128)S(1)} %get-tuple-element.59), channel_id=1, source_target_pairs={{0,3},{1,0},{2,1},{3,2},{4,7},{5,4},{6,5},{7,6},{8,11},{9,8},{10,9... | collective-permute-start | bytes 393224 | tf_op jit(solution)/shard_map/ppermute | solution.py:655
  19.9 1.3 %collective-permute-start.10 = (f32[38,1024]{1,0:T(8,128)S(1)}, f32[38,1024]{1,0:T(8,128)S(1)}, u32[]{:S(2)}, u32[]{:S(2)}) collective-permute-start(f32[38,1024]{1,0:T(8,128)S(1)} %get-tuple-element.65.refs_4_), channel_id=1, source_target_pairs={{3,1},{7,5},{11,9},{15,13},{19,17},{23,21},{27,25},{31,29}} | collective-permute-start | bytes 466952 | tf_op jit(solution)/shard_map/ppermute | solution.py:717
  21.2 1.3 %collective-permute-start.11 = (f32[38,1024]{1,0:T(8,128)S(1)}, f32[38,1024]{1,0:T(8,128)S(1)}, u32[]{:S(2)}, u32[]{:S(2)}) collective-permute-start(f32[38,1024]{1,0:T(8,128)S(1)} %get-tuple-element.65.refs_4_), channel_id=1, source_target_pairs={{2,1},{6,5},{10,9},{14,13},{18,17},{22,21},{26,25},{30,29}} | collective-permute-start | bytes 466952 | tf_op jit(solution)/shard_map/ppermute | solution.py:717
  22.5 3.7 %collective-permute-done.3.refs_5_ = f32[2,16,1024]{2,1,0:T(8,128)S(1)} collective-permute-done((f32[2,16,1024]{2,1,0:T(8,128)S(1)}, f32[2,16,1024]{2,1,0:T(8,128)S(1)}, u32[]{:S(2)}, u32[]{:S(2)}) %collective-permute-start.3) | collective-permute-done | bytes 131104 | tf_op jit(solution)/shard_map/ppermute | solution.py:655
  26.2 2.7 %collective-permute-start = (f32[2,16,1024]{2,1,0:T(8,128)S(1)}, f32[2,16,1024]{2,1,0:T(8,128)S(1)}, u32[]{:S(2)}, u32[]{:S(2)}) collective-permute-start(f32[2,16,1024]{2,1,0:T(8,128)S(1)} %get-tuple-element.50), channel_id=1, source_target_pairs={{0,1},{1,2},{2,3},{3,0},{4,5},{5,6},{6,7},{7,4},{8,9},{9,10},{10,1... | collective-permute-start | bytes 393224 | tf_op jit(solution)/shard_map/ppermute | solution.py:655
  28.9 0.3 collective-permute-done.4.refs_6_
  29.2 3.4 %collective-permute-start.1 = (f32[2,16,1024]{2,1,0:T(8,128)S(1)}, f32[2,16,1024]{2,1,0:T(8,128)S(1)}, u32[]{:S(2)}, u32[]{:S(2)}) collective-permute-start(f32[2,16,1024]{2,1,0:T(8,128)S(1)} %get-tuple-element.51), channel_id=1, source_target_pairs={{0,2},{1,3},{2,0},{3,1},{4,6},{5,7},{6,4},{7,5},{8,10},{9,11},{10,... | collective-permute-start | bytes 393224 | tf_op jit(solution)/shard_map/ppermute | solution.py:655
  32.6 6.5 %collective-permute-done.5.refs_7_ = f32[2,16,1024]{2,1,0:T(8,128)S(1)} collective-permute-done((f32[2,16,1024]{2,1,0:T(8,128)S(1)}, f32[2,16,1024]{2,1,0:T(8,128)S(1)}, u32[]{:S(2)}, u32[]{:S(2)}) %collective-permute-start.5) | collective-permute-done | bytes 131104 | tf_op jit(solution)/shard_map/ppermute | solution.py:655
  39.1 10.9 %compress.6 = (f32[2,32,1024]{2,1,0:T(8,128)S(1)}, f32[2,32,1024]{2,1,0:T(8,128)S(1)}, f32[2,32,1024]{2,1,0:T(8,128)S(1)}, f32[2,32,1024]{2,1,0:T(8,128)S(1)}) custom-call(s32[1]{0:T(128)} %bitcast.1.me_ref, bf16[2,1024,4096]{2,1,0:T(8,128)(2,1)S(1)} %get-tuple-element.53.x_ref, f32[2,32,128]{2,1,0:T(8,128)S(1)} %get-tuple-element.54.g_ref, ...), custom_call_target="tpu_custom_call" | custom-call | flops 17179869184 | bytes 16777216 | tf_op jit(solution)/shard_map/compress/pallas_call | solution.py:301
  50.0 1.3 %collective-permute-start.9 = (f32[38,1024]{1,0:T(8,128)S(1)}, f32[38,1024]{1,0:T(8,128)S(1)}, u32[]{:S(2)}, u32[]{:S(2)}) collective-permute-start(f32[38,1024]{1,0:T(8,128)S(1)} %get-tuple-element.65.refs_4_), channel_id=1, source_target_pairs={{0,1},{4,5},{8,9},{12,13},{16,17},{20,21},{24,25},{28,29}} | collective-permute-start | bytes 466952 | tf_op jit(solution)/shard_map/ppermute | solution.py:717
  51.3 1.5 %collective-permute-start.6 = (f32[2,32,1024]{2,1,0:T(8,128)S(1)}, f32[2,32,1024]{2,1,0:T(8,128)S(1)}, u32[]{:S(2)}, u32[]{:S(2)}) collective-permute-start(f32[2,32,1024]{2,1,0:T(8,128)S(1)} %get-tuple-element.62), channel_id=1, source_target_pairs={{0,1},{1,2},{2,3},{3,0},{4,5},{5,6},{6,7},{7,4},{8,9},{9,10},{10,1... | collective-permute-start | bytes 786440 | tf_op jit(solution)/shard_map/ppermute | solution.py:655
  52.8 3.6 %collective-permute-start.7 = (f32[2,32,1024]{2,1,0:T(8,128)S(1)}, f32[2,32,1024]{2,1,0:T(8,128)S(1)}, u32[]{:S(2)}, u32[]{:S(2)}) collective-permute-start(f32[2,32,1024]{2,1,0:T(8,128)S(1)} %get-tuple-element.63), channel_id=1, source_target_pairs={{0,2},{1,3},{2,0},{3,1},{4,6},{5,7},{6,4},{7,5},{8,10},{9,11},{10,... | collective-permute-start | bytes 786440 | tf_op jit(solution)/shard_map/ppermute | solution.py:655
  56.4 1.1 doppler.3
  57.5 0.1 collective-permute-start.8
  57.6 3.4 %collective-permute-start.15 = (f32[1216,128]{1,0:T(8,128)S(1)}, f32[1216,128]{1,0:T(8,128)S(1)}, u32[]{:S(2)}, u32[]{:S(2)}) collective-permute-start(f32[1216,128]{1,0:T(8,128)S(1)} %get-tuple-element.77), channel_id=1, source_target_pairs={{1,0},{3,2},{5,4},{7,6},{9,8},{11,10},{13,12},{15,14},{17,16},{19,... | collective-permute-start | bytes 1867784 | tf_op jit(solution)/shard_map/ppermute | solution.py:696
  61.0 0.0 copy-start.8
  61.0 0.0 copy-start.3
  61.0 0.0 copy-start.4
  61.0 10.9 %compress.7 = (f32[2,32,1024]{2,1,0:T(8,128)S(1)}, f32[2,32,1024]{2,1,0:T(8,128)S(1)}, f32[2,32,1024]{2,1,0:T(8,128)S(1)}, f32[2,32,1024]{2,1,0:T(8,128)S(1)}) custom-call(s32[1]{0:T(128)} %bitcast.1.me_ref, bf16[2,1024,4096]{2,1,0:T(8,128)(2,1)S(1)} %get-tuple-element.53.x_ref, f32[2,32,128]{2,1,0:T(8,128)S(1)} %get-tuple-element.54.g_ref, ...), custom_call_target="tpu_custom_call" | custom-call | flops 17179869184 | bytes 16777216 | tf_op jit(solution)/shard_map/compress/pallas_call | solution.py:301
  72.0 0.1 collective-permute-start.12
  72.1 2.1 %collective-permute-start.13 = (f32[2,32,1024]{2,1,0:T(8,128)S(1)}, f32[2,32,1024]{2,1,0:T(8,128)S(1)}, u32[]{:S(2)}, u32[]{:S(2)}) collective-permute-start(f32[2,32,1024]{2,1,0:T(8,128)S(1)} %get-tuple-element.72), channel_id=1, source_target_pairs={{0,2},{1,3},{2,0},{3,1},{4,6},{5,7},{6,4},{7,5},{8,10},{9,11},{10,... | collective-permute-start | bytes 786440 | tf_op jit(solution)/shard_map/ppermute | solution.py:655
  74.1 2.0 %collective-permute-done.7.refs_2_ = f32[2,32,1024]{2,1,0:T(8,128)S(1)} collective-permute-done((f32[2,32,1024]{2,1,0:T(8,128)S(1)}, f32[2,32,1024]{2,1,0:T(8,128)S(1)}, u32[]{:S(2)}, u32[]{:S(2)}) %collective-permute-start.7) | collective-permute-done | bytes 262176 | tf_op jit(solution)/shard_map/ppermute | solution.py:655
  77.4 0.1 broadcast_in_dim.8.fm_ref
  77.5 3.5 %phases.1 = (f32[2,32,40,128]{3,2,1,0:T(8,128)S(1)}, f32[2,32,32,128]{3,2,1,0:T(8,128)S(1)}, f32[2,32,24,128]{3,2,1,0:T(8,128)S(1)}, f32[256,128]{1,0:T(8,128)S(1)}) custom-call(f32[96,128]{1,0:T(8,128)S(1)} %broadcast_in_dim.8.fm_ref, f32[8,4096]{1,0:T(8,128)S(1)} %copy-done.3, f32[128,128]{1,0:T(8,128)S(1)} %copy-done.4), custom_call_target="tpu_custom_call" | custom-call | flops 23592960 | bytes 3145728 | tf_op jit(solution)/shard_map/phases/pallas_call | solution.py:461
  81.0 0.0 copy-start.2
  81.1 1.9 %doppler.4 = (f32[2,32,32,128]{3,2,1,0:T(8,128)S(1)}, f32[1216,128]{1,0:T(8,128)S(1)}) custom-call(s32[1]{0:T(128)} %bitcast.1.me_ref, f32[2,32,1024]{2,1,0:T(8,128)S(1)} %get-tuple-element.61.refs_0_.keep_ref, f32[2,32,1024]{2,1,0:T(8,128)S(1)} %collective-permute-done.6.refs_1_, f32[2,32,1024]{2,1,0:T(8,128)S(1)} %collective-permute-done.7.refs_2_, ...), custom_call_target="tpu_custom_call" | custom-call | flops 402653184 | bytes 2097152 | tf_op jit(solution)/shard_map/doppler/pallas_call | solution.py:385
  83.0 3.7 %focus.3 = (f32[2,40,4096]{2,1,0:T(8,128)S(1)}, f32[2,40,128]{2,1,0:T(8,128)S(1)}, f32[2,40,128]{2,1,0:T(8,128)S(1)}, f32[8,128]{1,0:T(8,128)S(1)}) custom-call(s32[96]{0:T(128)S(1)} %bitcast.3, s32[1]{0:T(128)} %bitcast.1.me_ref, f32[2,32,32,128]{3,2,1,0:T(8,128)S(1)} %get-tuple-element.60.refs_0_, ...), custom_call_target="tpu_custom_call" | custom-call | flops 503316480 | bytes 5242880 | tf_op jit(solution)/shard_map/focus/pallas_call | solution.py:567
  86.6 6.4 %collective-permute-done.12.refs_1_ = f32[2,32,1024]{2,1,0:T(8,128)S(1)} collective-permute-done((f32[2,32,1024]{2,1,0:T(8,128)S(1)}, f32[2,32,1024]{2,1,0:T(8,128)S(1)}, u32[]{:S(2)}, u32[]{:S(2)}) %collective-permute-start.12) | collective-permute-done | bytes 262176 | tf_op jit(solution)/shard_map/ppermute | solution.py:655
  93.0 6.4 %collective-permute-done.13.refs_2_ = f32[2,32,1024]{2,1,0:T(8,128)S(1)} collective-permute-done((f32[2,32,1024]{2,1,0:T(8,128)S(1)}, f32[2,32,1024]{2,1,0:T(8,128)S(1)}, u32[]{:S(2)}, u32[]{:S(2)}) %collective-permute-start.13) | collective-permute-done | bytes 262176 | tf_op jit(solution)/shard_map/ppermute | solution.py:655
  99.4 2.4 %collective-permute-done.14.refs_3_ = f32[2,32,1024]{2,1,0:T(8,128)S(1)} collective-permute-done((f32[2,32,1024]{2,1,0:T(8,128)S(1)}, f32[2,32,1024]{2,1,0:T(8,128)S(1)}, u32[]{:S(2)}, u32[]{:S(2)}) %collective-permute-start.14) | collective-permute-done | bytes 262176 | tf_op jit(solution)/shard_map/ppermute | solution.py:655
  101.8 1.1 doppler.5.refs_1_.refs_0_
  102.9 3.2 %focus.4 = (f32[2,32,4096]{2,1,0:T(8,128)S(1)}, f32[2,32,128]{2,1,0:T(8,128)S(1)}, f32[2,32,128]{2,1,0:T(8,128)S(1)}, f32[8,128]{1,0:T(8,128)S(1)}) custom-call(s32[96]{0:T(128)S(1)} %bitcast.4, s32[1]{0:T(128)} %bitcast.1.me_ref, f32[2,32,32,128]{3,2,1,0:T(8,128)S(1)} %get-tuple-element.67.refs_1_.refs_0_, f32[2,32,32,128]{3,2,1,0:T(8,128)S(1)} %doppler.5.refs_1_.refs_0_, ...), custom_call_target="tpu_custom_call" | custom-call | flops 402653184 | bytes 4194304 | tf_op jit(solution)/shard_map/focus/pallas_call | solution.py:567
  106.1 2.8 %focus.5 = (f32[2,24,4096]{2,1,0:T(8,128)S(1)}, f32[2,24,128]{2,1,0:T(8,128)S(1)}, f32[2,96,128]{2,1,0:T(8,128)S(1)}, f32[8,128]{1,0:T(8,128)S(1)}) custom-call(s32[96]{0:T(128)S(1)} %bitcast.5, s32[1]{0:T(128)} %bitcast.1.me_ref, f32[2,32,32,128]{3,2,1,0:T(8,128)S(1)} %doppler.5.refs_1_.refs_0_, f32[1216,128]{1,0:T(8,128)S(1)} %collective-permute-done.15.refs_1_, ...), custom_call_target="tpu_custom_call" | custom-call | flops 301989888 | bytes 3145728 | tf_op jit(solution)/shard_map/focus/pallas_call | solution.py:567
  108.9 1.9 %collective-permute-start.16 = (f32[2,96,128]{2,1,0:T(8,128)S(1)}, f32[2,96,128]{2,1,0:T(8,128)S(1)}, u32[]{:S(2)}, u32[]{:S(2)}) collective-permute-start(f32[2,96,128]{2,1,0:T(8,128)S(1)} %get-tuple-element.86), channel_id=1, source_target_pairs={{0,4},{4,8},{8,12},{12,16},{16,20},{20,24},{24,28},{1,5},{5,9},{9,... | collective-permute-start | bytes 294920 | tf_op jit(solution)/shard_map/ppermute | solution.py:750
  110.9 0.1 pad_add_fusion.seam_ref
  110.9 4.8 %collective-permute-done.16.refs_3_ = f32[2,96,128]{2,1,0:T(8,128)S(1)} collective-permute-done((f32[2,96,128]{2,1,0:T(8,128)S(1)}, f32[2,96,128]{2,1,0:T(8,128)S(1)}, u32[]{:S(2)}, u32[]{:S(2)}) %collective-permute-start.16) | collective-permute-done | bytes 98336 | tf_op jit(solution)/shard_map/ppermute | solution.py:750
  115.8 0.6 blend.1
  116.4 2.6 %collective-permute-start.17 = (f32[8,128]{1,0:T(8,128)S(1)}, f32[8,128]{1,0:T(8,128)S(1)}, u32[]{:S(2)}, u32[]{:S(2)}) collective-permute-start(f32[8,128]{1,0:T(8,128)S(1)} %get-tuple-element.92.refs_6_), channel_id=1, source_target_pairs={{0,1},{1,2},{2,3},{3,0},{4,5},{5,6},{6,7},{7,4},{8,9},{9,10},{10,1... | collective-permute-start | bytes 12296 | tf_op jit(solution)/shard_map/ppermute | solution.py:655
  119.0 2.3 %collective-permute-start.18 = (f32[8,128]{1,0:T(8,128)S(1)}, f32[8,128]{1,0:T(8,128)S(1)}, u32[]{:S(2)}, u32[]{:S(2)}) collective-permute-start(f32[8,128]{1,0:T(8,128)S(1)} %get-tuple-element.92.refs_6_), channel_id=1, source_target_pairs={{0,2},{1,3},{2,0},{3,1},{4,6},{5,7},{6,4},{7,5},{8,10},{9,11},{10,... | collective-permute-start | bytes 12296 | tf_op jit(solution)/shard_map/ppermute | solution.py:655
  121.3 2.2 %collective-permute-done.18.refs_8_ = f32[8,128]{1,0:T(8,128)S(1)} collective-permute-done((f32[8,128]{1,0:T(8,128)S(1)}, f32[8,128]{1,0:T(8,128)S(1)}, u32[]{:S(2)}, u32[]{:S(2)}) %collective-permute-start.18) | collective-permute-done | bytes 4128 | tf_op jit(solution)/shard_map/ppermute | solution.py:655
  123.5 1.4 %collective-permute-done.19.refs_9_ = f32[8,128]{1,0:T(8,128)S(1)} collective-permute-done((f32[8,128]{1,0:T(8,128)S(1)}, f32[8,128]{1,0:T(8,128)S(1)}, u32[]{:S(2)}, u32[]{:S(2)}) %collective-permute-start.19) | collective-permute-done | bytes 4128 | tf_op jit(solution)/shard_map/ppermute | solution.py:655
  124.9 1.6 %finish.1 = bf16[1,2,96,4096]{3,2,1,0:T(8,128)(2,1)} custom-call(f32[2,40,4096]{2,1,0:T(8,128)S(1)} %get-tuple-element.69.refs_0_, f32[2,32,4096]{2,1,0:T(8,128)S(1)} %get-tuple-element.76.refs_1_, f32[2,24,4096]{2,1,0:T(8,128)S(1)} %get-tuple-element.82.refs_2_, f32[2,40,128]{2,1,0:T(8,128)S(1)} %get-tuple-element.89.refs_3_, ...), custom_call_target="tpu_custom_call" | custom-call | tf_op jit(solution)/shard_map/finish/pallas_call | solution.py:644
  (25 shorter events, 0.1 us)
Async XLA Ops:
  0.0 0.8 copy-start.6
  0.8 1.0 copy-start.7
  15.3 10.9 %collective-permute-start.3 = (f32[2,16,1024]{2,1,0:T(8,128)S(1)}, f32[2,16,1024]{2,1,0:T(8,128)S(1)}, u32[]{:S(2)}, u32[]{:S(2)}) collective-permute-start(f32[2,16,1024]{2,1,0:T(8,128)S(1)} %get-tuple-element.57), channel_id=1, source_target_pairs={{0,1},{1,2},{2,3},{3,0},{4,5},{5,6},{6,7},{7,4},{8,9},{9,10},{10,1... | collective-permute-start | bytes 393224 | tf_op jit(solution)/shard_map/ppermute | solution.py:655
  16.9 12.3 %collective-permute-start.4 = (f32[2,16,1024]{2,1,0:T(8,128)S(1)}, f32[2,16,1024]{2,1,0:T(8,128)S(1)}, u32[]{:S(2)}, u32[]{:S(2)}) collective-permute-start(f32[2,16,1024]{2,1,0:T(8,128)S(1)} %get-tuple-element.58), channel_id=1, source_target_pairs={{0,2},{1,3},{2,0},{3,1},{4,6},{5,7},{6,4},{7,5},{8,10},{9,11},{10,... | collective-permute-start | bytes 393224 | tf_op jit(solution)/shard_map/ppermute | solution.py:655
  18.1 20.9 %collective-permute-start.5 = (f32[2,16,1024]{2,1,0:T(8,128)S(1)}, f32[2,16,1024]{2,1,0:T(8,128)S(1)}, u32[]{:S(2)}, u32[]{:S(2)}) collective-permute-start(f32[2,16,1024]{2,1,0:T(8,128)S(1)} %get-tuple-element.59), channel_id=1, source_target_pairs={{0,3},{1,0},{2,1},{3,2},{4,7},{5,4},{6,5},{7,6},{8,11},{9,8},{10,9... | collective-permute-start | bytes 393224 | tf_op jit(solution)/shard_map/ppermute | solution.py:655
  19.9 37.6 %collective-permute-start.10 = (f32[38,1024]{1,0:T(8,128)S(1)}, f32[38,1024]{1,0:T(8,128)S(1)}, u32[]{:S(2)}, u32[]{:S(2)}) collective-permute-start(f32[38,1024]{1,0:T(8,128)S(1)} %get-tuple-element.65.refs_4_), channel_id=1, source_target_pairs={{3,1},{7,5},{11,9},{15,13},{19,17},{23,21},{27,25},{31,29}} | collective-permute-start | bytes 466952 | tf_op jit(solution)/shard_map/ppermute | solution.py:717
  21.2 36.4 %collective-permute-start.11 = (f32[38,1024]{1,0:T(8,128)S(1)}, f32[38,1024]{1,0:T(8,128)S(1)}, u32[]{:S(2)}, u32[]{:S(2)}) collective-permute-start(f32[38,1024]{1,0:T(8,128)S(1)} %get-tuple-element.65.refs_4_), channel_id=1, source_target_pairs={{2,1},{6,5},{10,9},{14,13},{18,17},{22,21},{26,25},{30,29}} | collective-permute-start | bytes 466952 | tf_op jit(solution)/shard_map/ppermute | solution.py:717
  26.2 23.8 %collective-permute-start = (f32[2,16,1024]{2,1,0:T(8,128)S(1)}, f32[2,16,1024]{2,1,0:T(8,128)S(1)}, u32[]{:S(2)}, u32[]{:S(2)}) collective-permute-start(f32[2,16,1024]{2,1,0:T(8,128)S(1)} %get-tuple-element.50), channel_id=1, source_target_pairs={{0,1},{1,2},{2,3},{3,0},{4,5},{5,6},{6,7},{7,4},{8,9},{9,10},{10,1... | collective-permute-start | bytes 393224 | tf_op jit(solution)/shard_map/ppermute | solution.py:655
  29.2 22.1 %collective-permute-start.1 = (f32[2,16,1024]{2,1,0:T(8,128)S(1)}, f32[2,16,1024]{2,1,0:T(8,128)S(1)}, u32[]{:S(2)}, u32[]{:S(2)}) collective-permute-start(f32[2,16,1024]{2,1,0:T(8,128)S(1)} %get-tuple-element.51), channel_id=1, source_target_pairs={{0,2},{1,3},{2,0},{3,1},{4,6},{5,7},{6,4},{7,5},{8,10},{9,11},{10,... | collective-permute-start | bytes 393224 | tf_op jit(solution)/shard_map/ppermute | solution.py:655
  39.0 13.7 %collective-permute-start.2 = (f32[2,16,1024]{2,1,0:T(8,128)S(1)}, f32[2,16,1024]{2,1,0:T(8,128)S(1)}, u32[]{:S(2)}, u32[]{:S(2)}) collective-permute-start(f32[2,16,1024]{2,1,0:T(8,128)S(1)} %get-tuple-element.52), channel_id=1, source_target_pairs={{0,3},{1,0},{2,1},{3,2},{4,7},{5,4},{6,5},{7,6},{8,11},{9,8},{10,9... | collective-permute-start | bytes 393224 | tf_op jit(solution)/shard_map/ppermute | solution.py:655
  39.0 17.3 %copy-start = (bf16[512,256]{1,0:T(8,128)(2,1)S(1)}, bf16[512,256]{1,0:T(8,128)(2,1)}, u32[]{:S(2)}) copy-start(bf16[512,256]{1,0:T(8,128)(2,1)} %constant.16.clone.refs_9_.refs_5_.refs_6_) | copy-start | bytes 786436
  39.1 17.3 %copy-start.1 = (f32[4,2,32,128]{3,2,1,0:T(8,128)S(1)}, f32[4,2,32,128]{3,2,1,0:T(8,128)}, u32[]{:S(2)}) copy-start(f32[4,2,32,128]{3,2,1,0:T(8,128)} %constant.15.clone.refs_8_.refs_4_) | copy-start | bytes 393220
  50.0 22.0 %collective-permute-start.9 = (f32[38,1024]{1,0:T(8,128)S(1)}, f32[38,1024]{1,0:T(8,128)S(1)}, u32[]{:S(2)}, u32[]{:S(2)}) collective-permute-start(f32[38,1024]{1,0:T(8,128)S(1)} %get-tuple-element.65.refs_4_), channel_id=1, source_target_pairs={{0,1},{4,5},{8,9},{12,13},{16,17},{20,21},{24,25},{28,29}} | collective-permute-start | bytes 466952 | tf_op jit(solution)/shard_map/ppermute | solution.py:717
  51.3 20.7 %collective-permute-start.6 = (f32[2,32,1024]{2,1,0:T(8,128)S(1)}, f32[2,32,1024]{2,1,0:T(8,128)S(1)}, u32[]{:S(2)}, u32[]{:S(2)}) collective-permute-start(f32[2,32,1024]{2,1,0:T(8,128)S(1)} %get-tuple-element.62), channel_id=1, source_target_pairs={{0,1},{1,2},{2,3},{3,0},{4,5},{5,6},{6,7},{7,4},{8,9},{9,10},{10,1... | collective-permute-start | bytes 786440 | tf_op jit(solution)/shard_map/ppermute | solution.py:655
  52.8 23.4 %collective-permute-start.7 = (f32[2,32,1024]{2,1,0:T(8,128)S(1)}, f32[2,32,1024]{2,1,0:T(8,128)S(1)}, u32[]{:S(2)}, u32[]{:S(2)}) collective-permute-start(f32[2,32,1024]{2,1,0:T(8,128)S(1)} %get-tuple-element.63), channel_id=1, source_target_pairs={{0,2},{1,3},{2,0},{3,1},{4,6},{5,7},{6,4},{7,5},{8,10},{9,11},{10,... | collective-permute-start | bytes 786440 | tf_op jit(solution)/shard_map/ppermute | solution.py:655
  57.5 23.5 %collective-permute-start.8 = (f32[2,32,1024]{2,1,0:T(8,128)S(1)}, f32[2,32,1024]{2,1,0:T(8,128)S(1)}, u32[]{:S(2)}, u32[]{:S(2)}) collective-permute-start(f32[2,32,1024]{2,1,0:T(8,128)S(1)} %get-tuple-element.64), channel_id=1, source_target_pairs={{0,3},{1,0},{2,1},{3,2},{4,7},{5,4},{6,5},{7,6},{8,11},{9,8},{10,9... | collective-permute-start | bytes 786440 | tf_op jit(solution)/shard_map/ppermute | solution.py:655
  57.6 48.5 %collective-permute-start.15 = (f32[1216,128]{1,0:T(8,128)S(1)}, f32[1216,128]{1,0:T(8,128)S(1)}, u32[]{:S(2)}, u32[]{:S(2)}) collective-permute-start(f32[1216,128]{1,0:T(8,128)S(1)} %get-tuple-element.77), channel_id=1, source_target_pairs={{1,0},{3,2},{5,4},{7,6},{9,8},{11,10},{13,12},{15,14},{17,16},{19,... | collective-permute-start | bytes 1867784 | tf_op jit(solution)/shard_map/ppermute | solution.py:696
  61.0 16.4 %copy-start.8 = (f32[1,96]{1,0:T(1,128)S(1)}, f32[1,96]{1,0:T(1,128)}, u32[]{:S(2)}) copy-start(f32[1,96]{1,0:T(1,128)} %param.15) | copy-start | bytes 1156
  61.0 16.5 %copy-start.3 = (f32[8,4096]{1,0:T(8,128)S(1)}, f32[8,4096]{1,0:T(8,128)}, u32[]{:S(2)}) copy-start(f32[8,4096]{1,0:T(8,128)} %w_ref.1) | copy-start | bytes 393220
  61.0 16.5 %copy-start.4 = (f32[128,128]{1,0:T(8,128)S(1)}, f32[128,128]{1,0:T(8,128)}, u32[]{:S(2)}) copy-start(f32[128,128]{1,0:T(8,128)} %constant.17.clone.pick_ref) | copy-start | bytes 196612
  72.0 21.0 %collective-permute-start.12 = (f32[2,32,1024]{2,1,0:T(8,128)S(1)}, f32[2,32,1024]{2,1,0:T(8,128)S(1)}, u32[]{:S(2)}, u32[]{:S(2)}) collective-permute-start(f32[2,32,1024]{2,1,0:T(8,128)S(1)} %get-tuple-element.71), channel_id=1, source_target_pairs={{0,1},{1,2},{2,3},{3,0},{4,5},{5,6},{6,7},{7,4},{8,9},{9,10},{10,1... | collective-permute-start | bytes 786440 | tf_op jit(solution)/shard_map/ppermute | solution.py:655
  72.1 27.4 %collective-permute-start.13 = (f32[2,32,1024]{2,1,0:T(8,128)S(1)}, f32[2,32,1024]{2,1,0:T(8,128)S(1)}, u32[]{:S(2)}, u32[]{:S(2)}) collective-permute-start(f32[2,32,1024]{2,1,0:T(8,128)S(1)} %get-tuple-element.72), channel_id=1, source_target_pairs={{0,2},{1,3},{2,0},{3,1},{4,6},{5,7},{6,4},{7,5},{8,10},{9,11},{10,... | collective-permute-start | bytes 786440 | tf_op jit(solution)/shard_map/ppermute | solution.py:655
  76.1 25.7 %collective-permute-start.14 = (f32[2,32,1024]{2,1,0:T(8,128)S(1)}, f32[2,32,1024]{2,1,0:T(8,128)S(1)}, u32[]{:S(2)}, u32[]{:S(2)}) collective-permute-start(f32[2,32,1024]{2,1,0:T(8,128)S(1)} %get-tuple-element.73), channel_id=1, source_target_pairs={{0,3},{1,0},{2,1},{3,2},{4,7},{5,4},{6,5},{7,6},{8,11},{9,8},{10,9... | collective-permute-start | bytes 786440 | tf_op jit(solution)/shard_map/ppermute | solution.py:655
  81.0 1.9 %copy-start.2 = (f32[2,32,128]{2,1,0:T(8,128)S(1)}, f32[2,32,128]{2,1,0:T(8,128)}, u32[]{:S(2)}) copy-start(f32[2,32,128]{2,1,0:T(8,128)} %constant.18.clone.refs_4_.refs_5_) | copy-start | bytes 98308
  81.1 1.9 %copy-start.5 = (s32[1,96]{1,0:T(1,128)S(1)}, s32[1,96]{1,0:T(1,128)}, u32[]{:S(2)}) copy-start(s32[1,96]{1,0:T(1,128)} %param.16) | copy-start | bytes 1156
  108.9 6.8 %collective-permute-start.16 = (f32[2,96,128]{2,1,0:T(8,128)S(1)}, f32[2,96,128]{2,1,0:T(8,128)S(1)}, u32[]{:S(2)}, u32[]{:S(2)}) collective-permute-start(f32[2,96,128]{2,1,0:T(8,128)S(1)} %get-tuple-element.86), channel_id=1, source_target_pairs={{0,4},{4,8},{8,12},{12,16},{16,20},{20,24},{24,28},{1,5},{5,9},{9,... | collective-permute-start | bytes 294920 | tf_op jit(solution)/shard_map/ppermute | solution.py:750
  116.4 4.9 %collective-permute-start.17 = (f32[8,128]{1,0:T(8,128)S(1)}, f32[8,128]{1,0:T(8,128)S(1)}, u32[]{:S(2)}, u32[]{:S(2)}) collective-permute-start(f32[8,128]{1,0:T(8,128)S(1)} %get-tuple-element.92.refs_6_), channel_id=1, source_target_pairs={{0,1},{1,2},{2,3},{3,0},{4,5},{5,6},{6,7},{7,4},{8,9},{9,10},{10,1... | collective-permute-start | bytes 12296 | tf_op jit(solution)/shard_map/ppermute | solution.py:655
  119.0 4.5 %collective-permute-start.18 = (f32[8,128]{1,0:T(8,128)S(1)}, f32[8,128]{1,0:T(8,128)S(1)}, u32[]{:S(2)}, u32[]{:S(2)}) collective-permute-start(f32[8,128]{1,0:T(8,128)S(1)} %get-tuple-element.92.refs_6_), channel_id=1, source_target_pairs={{0,2},{1,3},{2,0},{3,1},{4,6},{5,7},{6,4},{7,5},{8,10},{9,11},{10,... | collective-permute-start | bytes 12296 | tf_op jit(solution)/shard_map/ppermute | solution.py:655
  121.3 3.6 %collective-permute-start.19 = (f32[8,128]{1,0:T(8,128)S(1)}, f32[8,128]{1,0:T(8,128)S(1)}, u32[]{:S(2)}, u32[]{:S(2)}) collective-permute-start(f32[8,128]{1,0:T(8,128)S(1)} %get-tuple-element.92.refs_6_), channel_id=1, source_target_pairs={{0,3},{1,0},{2,1},{3,2},{4,7},{5,4},{6,5},{7,6},{8,11},{9,8},{10,9... | collective-permute-start | bytes 12296 | tf_op jit(solution)/shard_map/ppermute | solution.py:655
